TPU v7x, 32 devices: a whole 2x2x4 slice. The times are simulated.
32 devices in a mesh: table: 4 (over y, core), batch: 8 (over z, x).
Axes of the slice: x: 2, y: 2, z: 4, core: 2. Of those that a mesh axis runs over, the one named last changes fastest.
Arguments:
- emb: bfloat16 [4, 262144, 128], P('table', 'batch'), may hold values from -6 to 6
- short_rows: int32 [192, 4, 32], P(('table', 'batch')), may hold values from 0 to 262143
- short_len: int32 [192, 4], P(('table', 'batch')), may hold values from 1 to 32
- short_sample: int32 [192, 4], P(('table', 'batch')), may hold values from 0 to 7, as said below
- long_rows: int32 [64, 4, 512], P(('table', 'batch')), may hold values from 0 to 262143, as said below
- long_len: int32 [64, 4], P(('table', 'batch')), may hold values from 33 to 500, as said below
- long_sample: int32 [64, 4], P(('table', 'batch')), may hold values from 0 to 7, as said below
Outputs:
- pooled: float32 [256, 4, 128], P(('table', 'batch'))
Inputs may be any that keep to these rules, and one draw needn't show every extreme that they name: For each block of 6 short bags and 2 long bags with the same j // 6 and j // 2, and each table, short_sample and long_sample together name each of the 8 samples exactly once. `long_sample`: see short_sample. `long_rows`: within one bag no row id stands more than 256 times among the first long_len positions, and in every draw some bag has a row id that stands exactly that often. `long_len`: in every draw some long bag has length 500.
All inputs are finite; a program needn't handle non-finite values.
Results may differ from a plain program's by a relative error of at most 0.0003.
Values sent between devices are 32-bit elements; how exact they have to be, the bound alone decides.
A program may use at most 64 MiB of HBM per device.

v0:
```python
import jax
import jax.numpy as jnp
from jax import lax
from jax.sharding import PartitionSpec as P

AXES = ("table", "batch")


def mask_rows(rows, lengths):
    place = lax.broadcasted_iota(jnp.int32, rows.shape, 2)
    return jnp.where(place < lengths[:, :, None], rows, -1)


def split_keys(keys, row_base, rows_dev):
    local = keys - row_base
    inside = (local >= 0) & (local < rows_dev)
    high = jnp.where(inside, local // 128, -1)
    low = jnp.where(inside, local % 128, -1)
    low_hot = (low[:, :, None] == lax.broadcasted_iota(jnp.int32, (1, 1, 128), 2)).astype(
        jnp.bfloat16
    )
    return high, low_hot


def count_block(high, low_hot, index, high_count):
    targets = index * high_count + lax.broadcasted_iota(jnp.int32, (1, 1, high_count), 2)
    high_hot = (high[:, :, None] == targets).astype(jnp.bfloat16)
    counts = jnp.einsum("bwh,bwl->bhl", high_hot, low_hot, preferred_element_type=jnp.float32)
    return counts.astype(jnp.bfloat16).reshape(high.shape[0], high_count * 128)


def pool_rows(short_keys, long_keys, table, row_base):
    rows_dev = table.shape[0]
    block = min(8192, rows_dev)
    high_count = block // 128
    short_split = split_keys(short_keys, row_base, rows_dev)
    long_split = split_keys(long_keys, row_base, rows_dev)
    bag_count = short_keys.shape[0] + long_keys.shape[0]

    def add_block(index, total):
        counts = jnp.concatenate(
            [
                count_block(*short_split, index, high_count),
                count_block(*long_split, index, high_count),
            ],
            axis=0,
        )
        piece = lax.dynamic_slice_in_dim(table, index * block, block, 0)
        return total + jnp.dot(counts, piece, preferred_element_type=jnp.float32)

    start = jnp.zeros((bag_count, table.shape[1]), jnp.float32)
    return lax.fori_loop(0, rows_dev // block, add_block, start)


def place_bags(values, lengths, samples, sample_count):
    scaled = values / jnp.sqrt(lengths.astype(jnp.float32))[:, :, None]
    slots = lax.broadcasted_iota(jnp.int32, samples.shape + (sample_count,), 2)
    picks = (samples[:, :, None] == slots).astype(jnp.float32)
    return jnp.sum(picks[:, :, :, None] * scaled[:, :, None, :], axis=0)


def on_device(emb, short_rows, short_len, short_sample, long_rows, long_len, long_sample):
    tables = lax.axis_size("table")
    batch = lax.axis_size("batch")
    devices = tables * batch
    short_dev, _, short_width = short_rows.shape
    long_dev, _, long_width = long_rows.shape
    width = emb.shape[2]
    short_flat = jnp.transpose(mask_rows(short_rows, short_len), (1, 0, 2)).reshape(tables, -1)
    long_flat = jnp.transpose(mask_rows(long_rows, long_len), (1, 0, 2)).reshape(tables, -1)
    keys = jnp.concatenate([short_flat, long_flat], axis=1)
    keys = jnp.broadcast_to(keys[:, None, :], (tables, batch, keys.shape[1]))
    keys = keys.reshape(devices, -1)
    keys = lax.all_to_all(keys, AXES, split_axis=0, concat_axis=0, tiled=True)
    short_all = keys[:, : short_dev * short_width].reshape(devices * short_dev, short_width)
    long_all = keys[:, short_dev * short_width :].reshape(devices * long_dev, long_width)
    row_base = lax.axis_index("batch") * emb.shape[1]
    part = pool_rows(short_all, long_all, emb[0], row_base)
    short_part = part[: devices * short_dev].reshape(devices, short_dev, width)
    long_part = part[devices * short_dev :].reshape(devices, long_dev, width)
    part = jnp.concatenate([short_part, long_part], axis=1)
    part = lax.all_to_all(part, AXES, split_axis=0, concat_axis=0, tiled=True)
    sums = jnp.sum(part.reshape(tables, batch, short_dev + long_dev, width), axis=1)
    sums = jnp.transpose(sums, (1, 0, 2))
    lengths = jnp.concatenate([short_len, long_len], axis=0)
    samples = jnp.concatenate([short_sample, long_sample], axis=0)
    pooled = place_bags(sums, lengths, samples, samples.shape[0])
    return jnp.transpose(pooled, (1, 0, 2))


def solution(mesh):
    return jax.shard_map(
        on_device,
        mesh=mesh,
        in_specs=(
            P("table", "batch", None),
            P(("table", "batch"), None, None),
            P(("table", "batch"), None),
            P(("table", "batch"), None),
            P(("table", "batch"), None, None),
            P(("table", "batch"), None),
            P(("table", "batch"), None),
        ),
        out_specs=P(("table", "batch"), None, None),
        check_vma=False,
    )
```

profile of v0, /device:TPU:0, one launch (start us, length us, event | category | flops | bytes accessed | tf_op | source)
XLA Modules:
  0.0 109.8 jit_solution(4178621504969128705)
XLA Ops:
  0.0 0.8 copy.27
  0.8 0.8 select_bitcast_fusion
  1.6 0.1 reshape.112
  1.6 0.8 fusion.47
  2.4 0.1 pad_add_fusion
  2.5 0.8 all_to_all.11
  3.4 7.3 %all-to-all-start = ((s32[32,1,1216]{2,1,0:T(1,128)}), s32[32,1,1216]{2,1,0:T(1,128)S(1)}, u32[]{:S(2)}, u32[]{:S(2)}) async-start(s32[32,1,1216]{2,1,0:T(1,128)} %all_to_all.11), calls=%async_computation | async-start | bytes 327680 | tf_op jit(solution)/shard_map/all_to_all | solution.py:74
  10.7 0.8 copy.29
  11.5 0.8 copy.25
  12.2 0.8 fusion.48
  13.0 5.7 %all-to-all-done = s32[32,1,1216]{2,1,0:T(1,128)S(1)} async-done(((s32[32,1,1216]{2,1,0:T(1,128)}), s32[32,1,1216]{2,1,0:T(1,128)S(1)}, u32[]{:S(2)}, u32[]{:S(2)}) %all-to-all-start) | async-done | bytes 155680 | tf_op jit(solution)/shard_map/all_to_all | solution.py:74
  18.7 0.1 slice_subtract_fusion
  18.9 0.1 fusion.39
  19.0 0.1 sub.40
  19.1 0.8 fusion.43
  19.9 0.0 copy-start
  19.9 77.7 %while.14 = (s32[]{:T(128)}, f32[256,128]{1,0:T(8,128)S(1)}, s32[192,32]{1,0:T(8,128)}, s32[64,512]{1,0:T(8,128)S(1)}, bf16[32768,128]{1,0:T(8,128)(2,1)}, /*ind...) while((s32[]{:T(128)}, f32[256,128]{1,0:T(8,128)S(1)}, ...), condition=%wide.region_1.2_spmd.clone, body=%wide.region_0.1_spmd.clone.sunk | while | flops 1197408256 | bytes 19448768 | solution.py:52
  19.9 6.1 %fusion.65 = bf16[192,64,128]{2,1,0:T(8,128)(2,1)S(1)} fusion(s32[192,32]{1,0:T(8,128)} %get-tuple-element.250, s32[64]{0:T(128)S(1)} %iota_add_fusion.2, s32[192,32]{1,0:T(8,128)} %get-tuple-element.247), kind=kOutput, calls=%fused_computation.18.clone.1 | convolution fusion | flops 104202240 | bytes 3195136 | tf_op jit(solution)/shard_map/while/body/eval_jaxpr/bwh,bwl->bhl/dot_general | solution.py:28
  26.0 2.8 %copy.44 = bf16[24,8,64,128]{3,1,2,0:T(8,128)(2,1)S(1)} copy(bf16[24,8,64,128]{3,2,1,0:T(8,128)(2,1)S(1)} %bitcast.32) | data formatting | bytes 6291456 | tf_op jit(solution)/shard_map/while
  28.8 5.5 %fusion.64 = bf16[64,64,128]{2,1,0:T(8,128)(2,1)S(1)} fusion(s32[64,512]{1,0:T(8,128)S(1)} %get-tuple-element.251, s32[64,512]{1,0:T(8,128)S(1)} %get-tuple-element.248, s32[64]{0:T(128)S(1)} %iota_add_fusion.2), kind=kOutput, calls=%fused_computation.23.clone.1 | convolution fusion | flops 547880960 | bytes 1310976 | tf_op jit(solution)/shard_map/while/body/eval_jaxpr/bwh,bwl->bhl/dot_general | solution.py:28
  34.3 1.7 %copy.43 = bf16[8,8,64,128]{3,1,2,0:T(8,128)(2,1)} copy(bf16[8,8,64,128]{3,2,1,0:T(8,128)(2,1)S(1)} %bitcast.34) | data formatting | bytes 2097152 | tf_op jit(solution)/shard_map/while
  36.0 3.2 %fusion.66 = f32[256,128]{1,0:T(8,128)S(1)} fusion(bf16[32768,128]{1,0:T(8,128)(2,1)} %get-tuple-element.249, s32[]{:T(128)S(6)} %select_n.98, bf16[64,8192]{1,0:T(8,128)(2,1)} %bitcast.33, bf16[192,8192]{1,0:T(8,128)(2,1)S(1)} %bitcast.31, f32[256,128]{1,0:T(8,128)S(1)} %get-tuple-element.234, pred[]{:T(512)S(6)} %compare.15), kind=kOutput, calls=%fused_computation.25.clone.1 | convolution fusion | flops 545325056 | bytes 6553605 | tf_op jit(solution)/shard_map/while/body/eval_jaxpr/dot_general | solution.py:49
  39.3 6.1 %fusion.65 = bf16[192,64,128]{2,1,0:T(8,128)(2,1)S(1)} fusion(s32[192,32]{1,0:T(8,128)} %get-tuple-element.250, s32[64]{0:T(128)S(1)} %iota_add_fusion.2, s32[192,32]{1,0:T(8,128)} %get-tuple-element.247), kind=kOutput, calls=%fused_computation.18.clone.1 | convolution fusion | flops 104202240 | bytes 3195136 | tf_op jit(solution)/shard_map/while/body/eval_jaxpr/bwh,bwl->bhl/dot_general | solution.py:28
  45.4 2.8 %copy.44 = bf16[24,8,64,128]{3,1,2,0:T(8,128)(2,1)S(1)} copy(bf16[24,8,64,128]{3,2,1,0:T(8,128)(2,1)S(1)} %bitcast.32) | data formatting | bytes 6291456 | tf_op jit(solution)/shard_map/while
  48.3 5.5 %fusion.64 = bf16[64,64,128]{2,1,0:T(8,128)(2,1)S(1)} fusion(s32[64,512]{1,0:T(8,128)S(1)} %get-tuple-element.251, s32[64,512]{1,0:T(8,128)S(1)} %get-tuple-element.248, s32[64]{0:T(128)S(1)} %iota_add_fusion.2), kind=kOutput, calls=%fused_computation.23.clone.1 | convolution fusion | flops 547880960 | bytes 1310976 | tf_op jit(solution)/shard_map/while/body/eval_jaxpr/bwh,bwl->bhl/dot_general | solution.py:28
  53.8 1.7 %copy.43 = bf16[8,8,64,128]{3,1,2,0:T(8,128)(2,1)} copy(bf16[8,8,64,128]{3,2,1,0:T(8,128)(2,1)S(1)} %bitcast.34) | data formatting | bytes 2097152 | tf_op jit(solution)/shard_map/while
  55.5 3.2 %fusion.66 = f32[256,128]{1,0:T(8,128)S(1)} fusion(bf16[32768,128]{1,0:T(8,128)(2,1)} %get-tuple-element.249, s32[]{:T(128)S(6)} %select_n.98, bf16[64,8192]{1,0:T(8,128)(2,1)} %bitcast.33, bf16[192,8192]{1,0:T(8,128)(2,1)S(1)} %bitcast.31, f32[256,128]{1,0:T(8,128)S(1)} %get-tuple-element.234, pred[]{:T(512)S(6)} %compare.15), kind=kOutput, calls=%fused_computation.25.clone.1 | convolution fusion | flops 545325056 | bytes 6553605 | tf_op jit(solution)/shard_map/while/body/eval_jaxpr/dot_general | solution.py:49
  58.7 6.1 %fusion.65 = bf16[192,64,128]{2,1,0:T(8,128)(2,1)S(1)} fusion(s32[192,32]{1,0:T(8,128)} %get-tuple-element.250, s32[64]{0:T(128)S(1)} %iota_add_fusion.2, s32[192,32]{1,0:T(8,128)} %get-tuple-element.247), kind=kOutput, calls=%fused_computation.18.clone.1 | convolution fusion | flops 104202240 | bytes 3195136 | tf_op jit(solution)/shard_map/while/body/eval_jaxpr/bwh,bwl->bhl/dot_general | solution.py:28
  64.8 2.8 %copy.44 = bf16[24,8,64,128]{3,1,2,0:T(8,128)(2,1)S(1)} copy(bf16[24,8,64,128]{3,2,1,0:T(8,128)(2,1)S(1)} %bitcast.32) | data formatting | bytes 6291456 | tf_op jit(solution)/shard_map/while
  67.7 5.5 %fusion.64 = bf16[64,64,128]{2,1,0:T(8,128)(2,1)S(1)} fusion(s32[64,512]{1,0:T(8,128)S(1)} %get-tuple-element.251, s32[64,512]{1,0:T(8,128)S(1)} %get-tuple-element.248, s32[64]{0:T(128)S(1)} %iota_add_fusion.2), kind=kOutput, calls=%fused_computation.23.clone.1 | convolution fusion | flops 547880960 | bytes 1310976 | tf_op jit(solution)/shard_map/while/body/eval_jaxpr/bwh,bwl->bhl/dot_general | solution.py:28
  73.2 1.7 %copy.43 = bf16[8,8,64,128]{3,1,2,0:T(8,128)(2,1)} copy(bf16[8,8,64,128]{3,2,1,0:T(8,128)(2,1)S(1)} %bitcast.34) | data formatting | bytes 2097152 | tf_op jit(solution)/shard_map/while
  74.9 3.2 %fusion.66 = f32[256,128]{1,0:T(8,128)S(1)} fusion(bf16[32768,128]{1,0:T(8,128)(2,1)} %get-tuple-element.249, s32[]{:T(128)S(6)} %select_n.98, bf16[64,8192]{1,0:T(8,128)(2,1)} %bitcast.33, bf16[192,8192]{1,0:T(8,128)(2,1)S(1)} %bitcast.31, f32[256,128]{1,0:T(8,128)S(1)} %get-tuple-element.234, pred[]{:T(512)S(6)} %compare.15), kind=kOutput, calls=%fused_computation.25.clone.1 | convolution fusion | flops 545325056 | bytes 6553605 | tf_op jit(solution)/shard_map/while/body/eval_jaxpr/dot_general | solution.py:49
  78.2 6.1 %fusion.65 = bf16[192,64,128]{2,1,0:T(8,128)(2,1)S(1)} fusion(s32[192,32]{1,0:T(8,128)} %get-tuple-element.250, s32[64]{0:T(128)S(1)} %iota_add_fusion.2, s32[192,32]{1,0:T(8,128)} %get-tuple-element.247), kind=kOutput, calls=%fused_computation.18.clone.1 | convolution fusion | flops 104202240 | bytes 3195136 | tf_op jit(solution)/shard_map/while/body/eval_jaxpr/bwh,bwl->bhl/dot_general | solution.py:28
  84.3 2.8 %copy.44 = bf16[24,8,64,128]{3,1,2,0:T(8,128)(2,1)S(1)} copy(bf16[24,8,64,128]{3,2,1,0:T(8,128)(2,1)S(1)} %bitcast.32) | data formatting | bytes 6291456 | tf_op jit(solution)/shard_map/while
  87.1 5.5 %fusion.64 = bf16[64,64,128]{2,1,0:T(8,128)(2,1)S(1)} fusion(s32[64,512]{1,0:T(8,128)S(1)} %get-tuple-element.251, s32[64,512]{1,0:T(8,128)S(1)} %get-tuple-element.248, s32[64]{0:T(128)S(1)} %iota_add_fusion.2), kind=kOutput, calls=%fused_computation.23.clone.1 | convolution fusion | flops 547880960 | bytes 1310976 | tf_op jit(solution)/shard_map/while/body/eval_jaxpr/bwh,bwl->bhl/dot_general | solution.py:28
  92.6 1.7 %copy.43 = bf16[8,8,64,128]{3,1,2,0:T(8,128)(2,1)} copy(bf16[8,8,64,128]{3,2,1,0:T(8,128)(2,1)S(1)} %bitcast.34) | data formatting | bytes 2097152 | tf_op jit(solution)/shard_map/while
  94.3 3.2 %fusion.66 = f32[256,128]{1,0:T(8,128)S(1)} fusion(bf16[32768,128]{1,0:T(8,128)(2,1)} %get-tuple-element.249, s32[]{:T(128)S(6)} %select_n.98, bf16[64,8192]{1,0:T(8,128)(2,1)} %bitcast.33, bf16[192,8192]{1,0:T(8,128)(2,1)S(1)} %bitcast.31, f32[256,128]{1,0:T(8,128)S(1)} %get-tuple-element.234, pred[]{:T(512)S(6)} %compare.15), kind=kOutput, calls=%fused_computation.25.clone.1 | convolution fusion | flops 545325056 | bytes 6553605 | tf_op jit(solution)/shard_map/while/body/eval_jaxpr/dot_general | solution.py:49
  97.6 0.7 pad_maximum_fusion
  98.3 2.9 %all-to-all-start.1 = ((f32[32,8,128]{2,1,0:T(8,128)}), f32[32,8,128]{2,1,0:T(8,128)S(1)}, u32[]{:S(2)}, u32[]{:S(2)}) async-start(f32[32,8,128]{2,1,0:T(8,128)} %pad_maximum_fusion), calls=%async_computation.1 | async-start | bytes 262144 | tf_op jit(solution)/shard_map/all_to_all | solution.py:82
  101.2 0.0 copy-done
  101.2 0.1 pad_add_fusion.1
  101.2 0.1 copy.26
  101.3 0.1 fusion.46
  101.4 7.6 %all-to-all-done.1 = f32[32,8,128]{2,1,0:T(8,128)S(1)} async-done(((f32[32,8,128]{2,1,0:T(8,128)}), f32[32,8,128]{2,1,0:T(8,128)S(1)}, u32[]{:S(2)}, u32[]{:S(2)}) %all-to-all-start.1) | async-done | bytes 131104 | tf_op jit(solution)/shard_map/all_to_all | solution.py:82
  109.0 0.1 bitcast_divide_fusion
  109.1 0.1 multiply_reduce_fusion
  109.2 0.6 copy.31
  (15 shorter events, 0.1 us)
Async XLA Ops:
  3.4 15.3 %all-to-all-start = ((s32[32,1,1216]{2,1,0:T(1,128)}), s32[32,1,1216]{2,1,0:T(1,128)S(1)}, u32[]{:S(2)}, u32[]{:S(2)}) async-start(s32[32,1,1216]{2,1,0:T(1,128)} %all_to_all.11), calls=%async_computation | async-start | bytes 327680 | tf_op jit(solution)/shard_map/all_to_all | solution.py:74
  19.9 81.3 %copy-start = (s32[6,4]{0,1:T(4,128)S(1)}, s32[6,4]{0,1:T(4,128)}, u32[]{:S(2)}) copy-start(s32[6,4]{0,1:T(4,128)} %param.12) | copy-start | bytes 292
  98.3 10.7 %all-to-all-start.1 = ((f32[32,8,128]{2,1,0:T(8,128)}), f32[32,8,128]{2,1,0:T(8,128)S(1)}, u32[]{:S(2)}, u32[]{:S(2)}) async-start(f32[32,8,128]{2,1,0:T(8,128)} %pad_maximum_fusion), calls=%async_computation.1 | async-start | bytes 262144 | tf_op jit(solution)/shard_map/all_to_all | solution.py:82
where the time goes:
time: 112 us; the launch traced here: 110 us
  matrix products  59.3 us (53%)
  local copies, waits for them, and re-layouts  22.3 us (20%)
  waiting for transfers between devices  13.3 us (12%)
  starting transfers between devices  10.2 us (9%)
  other arithmetic  4.45 us (4%)
    dot_general x8, matrix products, count_block(): jnp.einsum('bwh,bwl->bhl', high_hot, low_hot, preferred_element_type=jnp....  46.3 us
    while x8, local copies, waits for them, and re-layouts  18.2 us
    dot_general x4, matrix products, add_block(): return total + jnp.dot(counts, piece, preferred_element_type=jnp.float32)  13 us
    all_to_all x1, waiting for transfers between devices, on_device(): part = lax.all_to_all(part, AXES, split_axis=0, concat_axis=0, tiled=True)  7.56 us
    all_to_all x1, starting transfers between devices, on_device(): keys = lax.all_to_all(keys, AXES, split_axis=0, concat_axis=0, tiled=True)  7.33 us
    all_to_all x1, waiting for transfers between devices, on_device(): keys = lax.all_to_all(keys, AXES, split_axis=0, concat_axis=0, tiled=True)  5.7 us
    all_to_all x1, starting transfers between devices, on_device(): part = lax.all_to_all(part, AXES, split_axis=0, concat_axis=0, tiled=True)  2.85 us
    unnamed x6, local copies, waits for them, and re-layouts  2.31 us
  transfers between devices with their start and end apart: 2, of which 2 were waited for; matrix products, arithmetic and copies ran while one was open for 2% of the time, Pallas kernels for 0%

commit v1 on v0

v1 whole, which is shorter than its diff:
```python
import functools
import math

import jax
import jax.numpy as jnp
from jax import lax
from jax.experimental import pallas as pl
from jax.experimental.pallas import tpu as pltpu
from jax.sharding import PartitionSpec as P

MESH = pl.DeviceIdType.MESH
LANES = 128
GROUP = 8
EARLIER = 4096
TABLE_CHUNKS = 8
CONVERT_ROWS = 256


def capacity_of(short_dev, short_width, long_dev, long_width, batch):
    mean = (short_dev * short_width + long_dev * long_width) / batch
    slots = math.ceil((mean + 3.2 * math.sqrt(mean)) / 16) * 16
    return slots - 16 if slots % LANES == 0 else slots


def pool_kernel(
    tables,
    batch,
    slots,
    round_ref,
    emb_ref,
    short_rows_ref,
    short_len_ref,
    short_sample_ref,
    long_rows_ref,
    long_len_ref,
    long_sample_ref,
    out_ref,
    flag_ref,
    table_raw,
    table,
    long_ids,
    long_count,
    send_ids,
    send_weights,
    recv_ids,
    recv_weights,
    picked,
    send_sums,
    recv_sums,
    table_sems,
    own_sem,
    send_sems,
    ids_sems,
    weights_sems,
    sums_sem,
):
    devices = tables * batch
    short_dev, _, short_width = short_rows_ref.shape
    long_dev, _, long_width = long_rows_ref.shape
    rows_dev = table.shape[0]
    samples = out_ref.shape[0]
    halves = pl.cdiv(slots, LANES)
    groups = devices // GROUP
    my_table = lax.axis_index("table")
    my_batch = lax.axis_index("batch")
    me = my_table * batch + my_batch

    def peer(index):
        return (index // batch, index % batch)

    chunk = rows_dev // TABLE_CHUNKS

    def table_copy(index):
        span = pl.ds(index * chunk, chunk)
        return pltpu.make_async_copy(
            emb_ref.at[0, span, :], table_raw.at[span, :], table_sems.at[index]
        )

    for index in range(TABLE_CHUNKS):
        table_copy(index).start()

    barrier = pltpu.get_barrier_semaphore()

    def greet(step, _):
        pl.semaphore_signal(
            barrier, inc=1, device_id=peer((me + step) % devices), device_id_type=MESH
        )
        return 0

    lax.fori_loop(1, devices, greet, 0)

    pieces = long_width // LANES
    table_place = lax.broadcasted_iota(jnp.int32, (tables, long_width), 0)
    place = lax.broadcasted_iota(jnp.int32, (tables, long_width), 1)
    for bag in range(long_dev):
        lengths = jnp.zeros((tables, long_width), jnp.int32)
        for k in range(tables):
            lengths = jnp.where(table_place == k, long_len_ref[bag, k], lengths)
        masked = jnp.where(place < lengths, long_rows_ref[bag], -1)
        for c in range(pieces):
            long_ids[pl.ds(bag * tables, tables), c, :] = masked[:, c * LANES : (c + 1) * LANES]

    sub8 = lax.broadcasted_iota(jnp.int32, (8, LANES), 0)
    lane8 = lax.broadcasted_iota(jnp.int32, (8, LANES), 1)

    def merge(bag, _):
        row = long_ids[bag]
        parts = [row[c : c + 1, :] for c in range(pieces)]
        wide = [jnp.broadcast_to(part, (8, LANES)) for part in parts]
        total = [jnp.zeros((8, LANES), jnp.int32) for _ in range(pieces)]
        for c in range(pieces):
            column = jnp.broadcast_to(parts[c], (LANES, LANES)).T
            for g in range(LANES // 8):
                other = column[g * 8 : (g + 1) * 8, :]
                diagonal = jnp.where(sub8 + g * 8 < lane8, EARLIER + 1, 1)
                for e in range(pieces):
                    weight = diagonal if e == c else (EARLIER + 1 if c < e else 1)
                    total[e] = total[e] + jnp.where(other == wide[e], weight, 0)
        for e in range(pieces):
            seen = jnp.sum(total[e], axis=0, keepdims=True)
            keep = (seen < EARLIER) & (parts[e] >= 0)
            long_count[bag, pl.ds(e, 1), :] = jnp.where(keep, seen, 0)
        return 0

    lax.fori_loop(0, long_dev * tables, merge, 0)

    skipped = (round_ref[0] * slots).astype(jnp.float32)
    lane1 = lax.broadcasted_iota(jnp.int32, (1, LANES), 1)
    shard_base = lax.broadcasted_iota(jnp.int32, (batch, LANES), 0) * rows_dev
    slot_column = lax.broadcasted_iota(jnp.int32, (LANES, LANES), 0)
    first = lax.broadcasted_iota(jnp.int32, (LANES, 2 * LANES), 0)
    second = lax.broadcasted_iota(jnp.int32, (LANES, 2 * LANES), 1)
    prefix = ((first < second) | (second >= LANES)).astype(jnp.float32).astype(jnp.bfloat16)
    per_chunk = LANES // short_width
    short_chunks = pl.cdiv(short_dev, per_chunk)
    short_planes = []
    for c in range(short_chunks):
        planes = [
            short_rows_ref[c * per_chunk + i]
            if c * per_chunk + i < short_dev
            else jnp.full((tables, short_width), -1, jnp.int32)
            for i in range(per_chunk)
        ]
        short_planes.append(jnp.concatenate(planes, axis=1))

    over = jnp.zeros((batch, LANES), jnp.float32)
    results = []
    for k in range(tables):
        entries = []
        for bag in range(long_dev):
            for c in range(pieces):
                at = (bag * tables + k, slice(c, c + 1), slice(None))
                sample = jnp.full((1, LANES), long_sample_ref[bag, k], jnp.int32)
                entries.append((long_ids[at], long_count[at], sample))
        for c in range(short_chunks):
            lengths = jnp.zeros((1, LANES), jnp.int32)
            sample = jnp.zeros((1, LANES), jnp.int32)
            for i in range(per_chunk):
                bag = c * per_chunk + i
                if bag < short_dev:
                    mine = lane1 // short_width == i
                    lengths = jnp.where(mine, short_len_ref[bag, k], lengths)
                    sample = jnp.where(mine, short_sample_ref[bag, k], sample)
            count = jnp.where(lane1 % short_width < lengths, 1, 0)
            entries.append((short_planes[c][k : k + 1, :], count, sample))

        inside, local = [], []
        for ids, count, _ in entries:
            here = ids - shard_base
            local.append(here)
            inside.append((here >= 0) & (here < rows_dev) & (count > 0))
        marks = jnp.concatenate(
            [jnp.where(m, 1.0, 0.0).astype(jnp.float32) for m in inside], axis=0
        ).astype(jnp.bfloat16)
        ranks = jnp.dot(marks, prefix, preferred_element_type=jnp.float32)
        offset = jnp.zeros((batch, LANES), jnp.float32) - skipped
        left, right = [], []
        for c, (_, count, sample) in enumerate(entries):
            block = ranks[c * batch : (c + 1) * batch, :]
            rank = block[:, :LANES] + offset
            offset = offset + block[:, LANES:]
            over = jnp.maximum(over, jnp.where(inside[c] & (rank >= slots), 1.0, 0.0))
            target = jnp.zeros((batch, LANES), jnp.float32)
            masks = []
            for h in range(halves):
                top = min(slots, (h + 1) * LANES)
                mask = inside[c] & (rank >= h * LANES) & (rank < top)
                masks.append(mask)
                target = jnp.where(mask, rank - h * LANES, target)
            target = jnp.sum(target, axis=0, keepdims=True).astype(jnp.int32)
            right.append(
                jnp.where(slot_column == target, 1.0, 0.0).astype(jnp.bfloat16)
            )
            values = [
                (local[c] >> 8).astype(jnp.float32),
                (local[c] & 255).astype(jnp.float32),
                jnp.broadcast_to(sample.astype(jnp.float32), (batch, LANES)),
                jnp.broadcast_to(count.astype(jnp.float32), (batch, LANES)),
            ]
            left.append(
                jnp.concatenate(
                    [jnp.where(m, v, 0.0) for v in values for m in masks], axis=0
                ).astype(jnp.bfloat16)
            )
        results.append(
            lax.dot_general(
                jnp.concatenate(left, axis=1),
                jnp.concatenate(right, axis=1),
                (((1,), (1,)), ((), ())),
                preferred_element_type=jnp.float32,
            )
        )

    overflow = jnp.max(over, axis=(0, 1), keepdims=True).astype(jnp.int32)
    for k in range(tables):
        values = [
            [results[k][(p * halves + h) * batch :][:batch] for h in range(halves)]
            for p in range(4)
        ]
        span = pl.ds(k * batch, batch)
        for h in range(halves):
            ids = (values[0][h] * 256.0 + values[1][h]).astype(jnp.int32)
            send_ids[span, h, :] = jnp.clip(ids, 0, rows_dev - 1)
            send_weights[span, h, :] = values[2][h].astype(jnp.int32)
            count = values[3][h].astype(jnp.int32)
            if h == halves - 1:
                count = jnp.where(lane1 == LANES - 1, overflow, count)
            send_weights[span, halves + h, :] = count

    pl.semaphore_wait(barrier, devices - 1)

    def ids_copy(step):
        target = (me + step) % devices
        return pltpu.make_async_remote_copy(
            src_ref=send_ids.at[target],
            dst_ref=recv_ids.at[step],
            send_sem=send_sems.at[0],
            recv_sem=ids_sems.at[step // GROUP],
            device_id=peer(target),
            device_id_type=MESH,
        )

    def weights_copy(step):
        target = (me + step) % devices
        return pltpu.make_async_remote_copy(
            src_ref=send_weights.at[target],
            dst_ref=recv_weights.at[step],
            send_sem=send_sems.at[1],
            recv_sem=weights_sems.at[step // GROUP],
            device_id=peer(target),
            device_id_type=MESH,
        )

    own_ids = pltpu.make_async_copy(send_ids.at[me], recv_ids.at[0], own_sem)
    own_ids.start()
    recv_weights[0] = send_weights[me]

    def send(step, _):
        ids_copy(step).start()
        weights_copy(step).start()
        return 0

    lax.fori_loop(1, devices, send, 0)

    for index in range(TABLE_CHUNKS):
        table_copy(index).wait()

        def widen(step, _):
            span = pl.ds(
                pl.multiple_of(index * chunk + step * CONVERT_ROWS, CONVERT_ROWS), CONVERT_ROWS
            )
            table[span, :] = table_raw[span, :].astype(jnp.float32)
            return 0

        lax.fori_loop(0, chunk // CONVERT_ROWS, widen, 0)

    own_ids.wait()

    sample_rows = lax.broadcasted_iota(jnp.int32, (samples, LANES), 0)
    for group in range(groups):
        begin = group * GROUP
        arriving = GROUP - 1 if group == 0 else GROUP
        pltpu.make_async_copy(
            recv_ids.at[pl.ds(0, arriving)], recv_ids.at[pl.ds(0, arriving)], ids_sems.at[group]
        ).wait()

        def pick(step, _):
            for slot in range(slots):
                row = recv_ids[begin + step, slot // LANES, slot % LANES]
                picked[step, pl.ds(slot, 1), :] = table[pl.ds(row, 1), :]
            return 0

        lax.fori_loop(0, GROUP, pick, 0)
        pltpu.make_async_copy(
            recv_weights.at[pl.ds(0, arriving)],
            recv_weights.at[pl.ds(0, arriving)],
            weights_sems.at[group],
        ).wait()
        for step in range(GROUP):
            weights = []
            for h in range(halves):
                sample = recv_weights[begin + step, pl.ds(h, 1), :]
                count = recv_weights[begin + step, pl.ds(halves + h, 1), :]
                weight = jnp.where(sample_rows == sample, count, 0).astype(jnp.float32)
                weights.append(weight[:, : min(LANES, slots - h * LANES)])
            send_sums[begin + step] = jnp.dot(
                jnp.concatenate(weights, axis=1).astype(jnp.bfloat16),
                picked[step].astype(jnp.bfloat16),
                preferred_element_type=jnp.float32,
            )

        def answer(step, _):
            target = (me - step + devices) % devices
            pltpu.make_async_remote_copy(
                src_ref=send_sums.at[step],
                dst_ref=recv_sums.at[me],
                send_sem=send_sems.at[2],
                recv_sem=sums_sem,
                device_id=peer(target),
                device_id_type=MESH,
            ).start()
            return 0

        if group == 0:
            recv_sums[me] = send_sums[0]
        lax.fori_loop(max(begin, 1), begin + GROUP, answer, 0)

    others = pl.ds(0, devices - 1)
    pltpu.make_async_copy(recv_sums.at[others], recv_sums.at[others], sums_sem).wait()

    last = recv_weights[0, pl.ds(2 * halves - 1, 1), :]
    for step in range(1, devices):
        last = jnp.maximum(last, recv_weights[step, pl.ds(2 * halves - 1, 1), :])
    flag_ref[0] = jnp.max(jnp.where(lane1 == LANES - 1, last, 0))

    for k in range(tables):
        total = recv_sums[k * batch]
        for s in range(1, batch):
            total = total + recv_sums[k * batch + s]
        lengths = jnp.zeros((samples, LANES), jnp.int32)
        for bag in range(short_dev):
            lengths = jnp.where(
                sample_rows == short_sample_ref[bag, k], short_len_ref[bag, k], lengths
            )
        for bag in range(long_dev):
            lengths = jnp.where(
                sample_rows == long_sample_ref[bag, k], long_len_ref[bag, k], lengths
            )
        out_ref[:, k, :] = total / jnp.sqrt(lengths.astype(jnp.float32))

    pltpu.make_async_copy(send_ids.at[others], send_ids.at[others], send_sems.at[0]).wait()
    pltpu.make_async_copy(
        send_weights.at[others], send_weights.at[others], send_sems.at[1]
    ).wait()
    pltpu.make_async_copy(send_sums.at[others], send_sums.at[others], send_sems.at[2]).wait()


def on_device(emb, short_rows, short_len, short_sample, long_rows, long_len, long_sample):
    tables = lax.axis_size("table")
    batch = lax.axis_size("batch")
    devices = tables * batch
    short_dev, _, short_width = short_rows.shape
    long_dev, _, long_width = long_rows.shape
    rows_dev, width = emb.shape[1:]
    samples = short_dev + long_dev
    slots = capacity_of(short_dev, short_width, long_dev, long_width, batch)
    halves = pl.cdiv(slots, LANES)
    assert width == LANES and rows_dev <= 65536 and rows_dev % (TABLE_CHUNKS * CONVERT_ROWS) == 0
    assert long_width % LANES == 0 and long_width < EARLIER and LANES % short_width == 0
    assert devices % GROUP == 0

    smem = pl.BlockSpec(memory_space=pltpu.SMEM)
    vmem = pl.BlockSpec(memory_space=pltpu.VMEM)
    call = pl.pallas_call(
        functools.partial(pool_kernel, tables, batch, slots),
        out_shape=(
            jax.ShapeDtypeStruct((samples, tables, width), jnp.float32),
            jax.ShapeDtypeStruct((1,), jnp.int32),
        ),
        in_specs=[smem, pl.BlockSpec(memory_space=pl.ANY), vmem, smem, smem, vmem, smem, smem],
        out_specs=(vmem, smem),
        scratch_shapes=[
            pltpu.VMEM((rows_dev, width), jnp.bfloat16),
            pltpu.VMEM((rows_dev, width), jnp.float32),
            pltpu.VMEM((long_dev * tables, long_width // LANES, LANES), jnp.int32),
            pltpu.VMEM((long_dev * tables, long_width // LANES, LANES), jnp.int32),
            pltpu.VMEM((devices, halves, LANES), jnp.int32),
            pltpu.VMEM((devices, 2 * halves, LANES), jnp.int32),
            pltpu.SMEM((devices, halves, LANES), jnp.int32),
            pltpu.VMEM((devices, 2 * halves, LANES), jnp.int32),
            pltpu.VMEM((GROUP, slots, width), jnp.float32),
            pltpu.VMEM((devices, samples, width), jnp.float32),
            pltpu.VMEM((devices, samples, width), jnp.float32),
            pltpu.SemaphoreType.DMA((TABLE_CHUNKS,)),
            pltpu.SemaphoreType.DMA,
            pltpu.SemaphoreType.DMA((3,)),
            pltpu.SemaphoreType.DMA((devices // GROUP,)),
            pltpu.SemaphoreType.DMA((devices // GROUP,)),
            pltpu.SemaphoreType.DMA,
        ],
        compiler_params=pltpu.CompilerParams(
            collective_id=0, has_side_effects=True, vmem_limit_bytes=56 * 2**20
        ),
        name="pool",
    )

    def run(index):
        return call(
            jnp.full((1,), index, jnp.int32),
            emb,
            short_rows,
            short_len,
            short_sample,
            long_rows,
            long_len,
            long_sample,
        )

    rounds = pl.cdiv(short_dev * short_width + long_dev * long_width, slots)
    pooled, flag = run(0)
    return lax.cond(
        flag[0] > 0,
        lambda value: lax.fori_loop(1, rounds, lambda r, acc: acc + run(r)[0], value),
        lambda value: value,
        pooled,
    )


def solution(mesh):
    return jax.shard_map(
        on_device,
        mesh=mesh,
        in_specs=(
            P("table", "batch", None),
            P(("table", "batch"), None, None),
            P(("table", "batch"), None),
            P(("table", "batch"), None),
            P(("table", "batch"), None, None),
            P(("table", "batch"), None),
            P(("table", "batch"), None),
        ),
        out_specs=P(("table", "batch"), None, None),
        check_vma=False,
    )
```

time: 112 us -> 27.6 us (0.25)
  the two profiles are of different devices: /device:TPU:0 before, /device:TPU:1 now
where the time goes in v1:
time: 27.6 us; the launch traced here: 27.4 us
  Pallas kernels  23.2 us (84%)
  local copies, waits for them, and re-layouts  3.39 us (12%)
  between operations  0.72 us (3%)
    pallas_call x1, Pallas kernels, run(): call(jnp.full((1,), index, jnp.int32), emb, short_rows, short_len, short_...  23.2 us
    unnamed x15, local copies, waits for them, and re-layouts  3.39 us

profile of v1, /device:TPU:1, one launch (start us, length us, event | category | flops | bytes accessed | tf_op | source)
XLA Modules:
  0.0 27.4 jit_solution(11503112043420614328)
XLA Ops:
  0.0 0.0 copy-start.3
  0.0 0.0 copy-start.2
  0.0 0.0 copy-start
  0.0 0.0 copy-start.5
  0.0 0.0 copy-start.4
  0.0 0.0 copy-start.1
  0.0 1.4 %copy.10.short_len_ref = s32[6,4]{1,0:T(8,128)} copy(s32[6,4]{0,1:T(4,128)} %param.13) | data formatting | bytes 192 | tf_op args[2]
  1.4 1.4 %copy.11.short_sample_ref = s32[6,4]{1,0:T(8,128)} copy(s32[6,4]{0,1:T(4,128)} %param.14) | data formatting | bytes 192 | tf_op args[3]
  2.8 23.2 %pool.6 = (f32[8,4,128]{2,1,0:T(4,128)S(1)}, s32[1]{0:T(128)}) custom-call(s32[1]{0:T(128)} %constant.16.clone.1.round_ref, bf16[1,32768,128]{2,1,0:T(8,128)(2,1)} %emb_ref.1, s32[6,4,32]{2,1,0:T(4,128)} %short_rows_ref.1, s32[6,4]{1,0:T(8,128)} %copy.10.short_len_ref, s32[6,4]{1,0:T(8,128)} %copy.11.short_sample_ref, s32[2,4,512]{2,1,0:T(4,128)} %long_rows_ref.1, ...), custom_call_target="tpu_custom_call" | custom-call | tf_op jit(solution)/shard_map/pool/pallas_call | solution.py:408
  26.7 0.0 copy-done.3
  26.7 0.0 copy-done.2
  26.7 0.0 copy-done
  26.7 0.0 copy-done.5
  26.7 0.0 copy-done.4
  26.7 0.0 copy-done.1
  26.8 0.6 %copy.25 = f32[8,4,128]{2,1,0:T(4,128)} copy(f32[8,4,128]{2,1,0:T(4,128)S(1)} %get-tuple-element.178) | data formatting | bytes 32768
  (1 shorter events, 0.0 us)
Async XLA Ops:
  0.0 26.7 %copy-start.3 = (s32[2,4]{1,0:T(2,128)S(1)}, s32[2,4]{1,0:T(2,128)}, u32[]{:S(2)}) copy-start(s32[2,4]{1,0:T(2,128)} %long_sample_ref.1) | copy-start | bytes 100
  0.0 26.7 %copy-start.2 = (s32[2,4]{1,0:T(2,128)S(1)}, s32[2,4]{1,0:T(2,128)}, u32[]{:S(2)}) copy-start(s32[2,4]{1,0:T(2,128)} %long_len_ref.1) | copy-start | bytes 100
  0.0 26.7 %copy-start = (s32[2,4,512]{2,1,0:T(4,128)S(1)}, s32[2,4,512]{2,1,0:T(4,128)}, u32[]{:S(2)}) copy-start(s32[2,4,512]{2,1,0:T(4,128)} %long_rows_ref.1) | copy-start | bytes 49156
  0.0 26.7 %copy-start.5 = (s32[6,4]{0,1:T(4,128)S(1)}, s32[6,4]{0,1:T(4,128)}, u32[]{:S(2)}) copy-start(s32[6,4]{0,1:T(4,128)} %param.14) | copy-start | bytes 292
  0.0 26.7 %copy-start.4 = (s32[6,4]{0,1:T(4,128)S(1)}, s32[6,4]{0,1:T(4,128)}, u32[]{:S(2)}) copy-start(s32[6,4]{0,1:T(4,128)} %param.13) | copy-start | bytes 292
  0.0 26.7 %copy-start.1 = (s32[6,4,32]{2,1,0:T(4,128)S(1)}, s32[6,4,32]{2,1,0:T(4,128)}, u32[]{:S(2)}) copy-start(s32[6,4,32]{2,1,0:T(4,128)} %short_rows_ref.1) | copy-start | bytes 9220

commit v2 on v1

v2 whole, which is shorter than its diff:
```python
import functools
import math

import jax
import jax.numpy as jnp
from jax import lax
from jax.experimental import pallas as pl
from jax.experimental.pallas import tpu as pltpu
from jax.sharding import PartitionSpec as P

MESH = pl.DeviceIdType.MESH
LANES = 128
GROUP = 8
TABLE_CHUNKS = 8
CONVERT_ROWS = 512


def capacity_of(short_dev, short_width, long_dev, long_width, batch):
    mean = (short_dev * short_width + long_dev * long_width) / batch
    slots = math.ceil((mean + 3.2 * math.sqrt(mean)) / 16) * 16
    return slots - 16 if slots % LANES == 0 else slots


def pool_kernel(
    tables,
    batch,
    slots,
    round_ref,
    emb_ref,
    short_rows_hbm,
    short_len_hbm,
    short_sample_hbm,
    long_rows_hbm,
    long_len_hbm,
    long_sample_hbm,
    out_ref,
    flag_ref,
    short_rows_ref,
    short_len_ref,
    short_sample_ref,
    long_rows_ref,
    long_len_ref,
    long_sample_ref,
    table_raw,
    table,
    send_ids,
    send_weights,
    recv_ids,
    recv_weights,
    picked,
    send_sums,
    recv_sums,
    input_sems,
    table_sems,
    send_sems,
    ids_sems,
    weights_sems,
    sums_sem,
):
    devices = tables * batch
    short_dev, _, short_width = short_rows_ref.shape
    long_dev, _, long_width = long_rows_ref.shape
    rows_dev = table.shape[0]
    samples = out_ref.shape[0]
    halves = pl.cdiv(slots, LANES)
    groups = devices // GROUP
    my_table = lax.axis_index("table")
    my_batch = lax.axis_index("batch")
    me = my_batch * tables + my_table

    def partner(step):
        return my_table ^ (step % tables), my_batch ^ (step // tables)

    chunk = rows_dev // TABLE_CHUNKS

    def table_copy(index):
        span = pl.ds(index * chunk, chunk)
        return pltpu.make_async_copy(
            emb_ref.at[0, span, :], table_raw.at[span, :], table_sems.at[index]
        )

    inputs = [
        pltpu.make_async_copy(source, target, input_sems.at[index])
        for index, (source, target) in enumerate(
            [
                (long_rows_hbm, long_rows_ref),
                (long_len_hbm, long_len_ref),
                (short_rows_hbm, short_rows_ref),
                (short_len_hbm, short_len_ref),
                (short_sample_hbm, short_sample_ref),
                (long_sample_hbm, long_sample_ref),
            ]
        )
    ]
    for copy in inputs:
        copy.start()
    barrier = pltpu.get_barrier_semaphore()
    for step in reversed(range(1, devices)):
        pl.semaphore_signal(barrier, inc=1, device_id=partner(step), device_id_type=MESH)
    for index in range(TABLE_CHUNKS):
        table_copy(index).start()
    for copy in inputs:
        copy.wait()

    pieces = long_width // LANES
    table_place = lax.broadcasted_iota(jnp.int32, (tables, long_width), 0)
    place = lax.broadcasted_iota(jnp.int32, (tables, long_width), 1)
    sub8 = lax.broadcasted_iota(jnp.int32, (8, LANES), 0)
    lane8 = lax.broadcasted_iota(jnp.int32, (8, LANES), 1)
    ones = jnp.ones((8, LANES), jnp.float32).astype(jnp.bfloat16)
    long_entries = [[] for _ in range(tables)]
    for bag in range(long_dev):
        lengths = jnp.zeros((tables, long_width), jnp.int32)
        for k in range(tables):
            lengths = jnp.where(table_place == k, long_len_ref[bag, k], lengths)
        masked = jnp.where(place < lengths, long_rows_ref[bag], -1)
        for k in range(tables):
            parts = [masked[k : k + 1, c * LANES : (c + 1) * LANES] for c in range(pieces)]
            wide = [jnp.broadcast_to(part, (8, LANES)) for part in parts]
            column = jnp.broadcast_to(parts[0], (LANES, LANES)).T
            before = [jnp.zeros((8, LANES), jnp.float32) for _ in range(pieces)]
            equal = []
            for g in range(LANES // 8):
                other = column[g * 8 : (g + 1) * 8, :]
                row = None
                for e in range(pieces):
                    same = jnp.where(other == wide[e], 1.0, 0.0)
                    row = same if row is None else row + same
                    if e == 0:
                        same = jnp.where(sub8 + g * 8 < lane8, same, 0.0)
                    before[e] = before[e] + same
                equal.append(row)
            count = lax.dot_general(
                ones,
                jnp.concatenate(equal, axis=0).astype(jnp.bfloat16),
                (((1,), (1,)), ((), ())),
                preferred_element_type=jnp.float32,
            )[0:1, :]
            sample = jnp.full((1, LANES), long_sample_ref[bag, k], jnp.int32).astype(jnp.float32)
            for e in range(pieces):
                keep = jnp.sum(before[e], axis=0, keepdims=True) < 0.5
                total = count if e == 0 else jnp.ones((1, LANES), jnp.float32)
                long_entries[k].append((parts[e], jnp.where(keep, total, 0.0), sample))

    skipped = (round_ref[0] * slots).astype(jnp.float32)
    lane1 = lax.broadcasted_iota(jnp.int32, (1, LANES), 1)
    shard_base = lax.broadcasted_iota(jnp.int32, (batch, LANES), 0) * rows_dev
    slot_column = lax.broadcasted_iota(jnp.int32, (LANES, LANES), 0)
    first = lax.broadcasted_iota(jnp.int32, (LANES, 2 * LANES), 0)
    second = lax.broadcasted_iota(jnp.int32, (LANES, 2 * LANES), 1)
    prefix = ((first < second) | (second >= LANES)).astype(jnp.float32).astype(jnp.bfloat16)
    per_chunk = LANES // short_width
    short_chunks = pl.cdiv(short_dev, per_chunk)
    short_planes = []
    for c in range(short_chunks):
        planes = [
            short_rows_ref[c * per_chunk + i]
            if c * per_chunk + i < short_dev
            else jnp.full((tables, short_width), -1, jnp.int32)
            for i in range(per_chunk)
        ]
        short_planes.append(jnp.concatenate(planes, axis=1))

    over = jnp.zeros((batch, LANES), jnp.float32)
    results = []
    for k in range(tables):
        entries = list(long_entries[k])
        for c in range(short_chunks):
            lengths = jnp.zeros((1, LANES), jnp.int32)
            sample = jnp.zeros((1, LANES), jnp.int32)
            for i in range(per_chunk):
                bag = c * per_chunk + i
                if bag < short_dev:
                    mine = lane1 // short_width == i
                    lengths = jnp.where(mine, short_len_ref[k, bag], lengths)
                    sample = jnp.where(mine, short_sample_ref[k, bag], sample)
            count = jnp.where(lane1 % short_width < lengths, 1.0, 0.0)
            entries.append((short_planes[c][k : k + 1, :], count, sample.astype(jnp.float32)))

        inside, local = [], []
        for ids, count, _ in entries:
            here = ids - shard_base
            local.append(here)
            inside.append((here >= 0) & (here < rows_dev) & (count > 0.0))
        marks = jnp.concatenate(
            [jnp.where(m, 1.0, 0.0).astype(jnp.float32) for m in inside], axis=0
        ).astype(jnp.bfloat16)
        ranks = jnp.dot(marks, prefix, preferred_element_type=jnp.float32)
        offset = jnp.zeros((batch, LANES), jnp.float32) - skipped
        left, right = [], []
        for c, (_, count, sample) in enumerate(entries):
            block = ranks[c * batch : (c + 1) * batch, :]
            rank = block[:, :LANES] + offset
            offset = offset + block[:, LANES:]
            over = jnp.maximum(over, jnp.where(inside[c] & (rank >= slots), 1.0, 0.0))
            target = jnp.zeros((batch, LANES), jnp.float32)
            masks = []
            for h in range(halves):
                top = min(slots, (h + 1) * LANES)
                mask = inside[c] & (rank >= h * LANES) & (rank < top)
                masks.append(mask)
                target = jnp.where(mask, rank - h * LANES, target)
            target = jnp.sum(target, axis=0, keepdims=True).astype(jnp.int32)
            right.append(jnp.where(slot_column == target, 1.0, 0.0).astype(jnp.bfloat16))
            values = [
                (local[c] >> 8).astype(jnp.float32),
                (local[c] & 255).astype(jnp.float32),
                jnp.broadcast_to(sample, (batch, LANES)),
                jnp.broadcast_to(count, (batch, LANES)),
            ]
            left.append(
                jnp.concatenate(
                    [jnp.where(m, v, 0.0) for v in values for m in masks], axis=0
                ).astype(jnp.bfloat16)
            )
        results.append(
            lax.dot_general(
                jnp.concatenate(left, axis=1),
                jnp.concatenate(right, axis=1),
                (((1,), (1,)), ((), ())),
                preferred_element_type=jnp.float32,
            )
        )

    overflow = jnp.max(over, axis=(0, 1), keepdims=True).astype(jnp.int32)
    for k in range(tables):
        values = [
            [results[k][(p * halves + h) * batch :][:batch] for h in range(halves)]
            for p in range(4)
        ]
        for h in range(halves):
            ids = (values[0][h] * 256.0 + values[1][h]).astype(jnp.int32)
            send_ids[:, k, h, :] = jnp.clip(ids, 0, rows_dev - 1)
            send_weights[:, k, h, :] = values[2][h].astype(jnp.int32)
            count = values[3][h].astype(jnp.int32)
            if h == halves - 1:
                count = jnp.where(lane1 == LANES - 1, overflow, count)
            send_weights[:, k, halves + h, :] = count

    pl.semaphore_wait(barrier, devices - 1)
    my_group = me // GROUP
    for step in reversed(range(1, devices)):
        to_table, to_batch = partner(step)
        pltpu.make_async_remote_copy(
            src_ref=send_ids.at[to_batch, to_table],
            dst_ref=recv_ids.at[me],
            send_sem=send_sems.at[0],
            recv_sem=ids_sems.at[my_group],
            device_id=(to_table, to_batch),
            device_id_type=MESH,
        ).start()
    pltpu.make_async_copy(
        send_ids.at[my_batch, my_table], recv_ids.at[me], ids_sems.at[my_group]
    ).start()
    for step in reversed(range(1, devices)):
        to_table, to_batch = partner(step)
        pltpu.make_async_remote_copy(
            src_ref=send_weights.at[to_batch, to_table],
            dst_ref=recv_weights.at[me],
            send_sem=send_sems.at[1],
            recv_sem=weights_sems.at[my_group],
            device_id=(to_table, to_batch),
            device_id_type=MESH,
        ).start()
    recv_weights[me] = send_weights[my_batch, my_table]

    for index in range(TABLE_CHUNKS):
        table_copy(index).wait()

        def widen(step, _):
            span = pl.ds(
                pl.multiple_of(index * chunk + step * CONVERT_ROWS, CONVERT_ROWS), CONVERT_ROWS
            )
            table[span, :] = table_raw[span, :].astype(jnp.float32)
            return 0

        lax.fori_loop(0, chunk // CONVERT_ROWS, widen, 0)

    def arrived(ref, sem, count):
        pltpu.make_async_copy(ref.at[pl.ds(0, count)], ref.at[pl.ds(0, count)], sem).wait()

    sample_rows = lax.broadcasted_iota(jnp.int32, (samples, LANES), 0)
    for group in range(groups):
        begin = group * GROUP
        arrived(recv_ids, ids_sems.at[group], GROUP)
        for step in range(GROUP):
            for slot in range(slots):
                row = recv_ids[begin + step, slot // LANES, slot % LANES]
                picked[group % 2, step, pl.ds(slot, 1), :] = table[pl.ds(row, 1), :]

        @pl.when(my_group == group)
        def _():
            arrived(recv_weights, weights_sems.at[group], GROUP - 1)

        @pl.when(my_group != group)
        def _():
            arrived(recv_weights, weights_sems.at[group], GROUP)

        for step in range(GROUP):
            weights = []
            for h in range(halves):
                sample = recv_weights[begin + step, pl.ds(h, 1), :]
                count = recv_weights[begin + step, pl.ds(halves + h, 1), :]
                weight = jnp.where(sample_rows == sample, count, 0).astype(jnp.float32)
                weights.append(weight[:, : min(LANES, slots - h * LANES)])
            send_sums[begin + step] = jnp.dot(
                jnp.concatenate(weights, axis=1).astype(jnp.bfloat16),
                picked[group % 2, step].astype(jnp.bfloat16),
                preferred_element_type=jnp.float32,
            )
        for step in range(GROUP):
            source = begin + step

            @pl.when(me != source)
            def _():
                pltpu.make_async_remote_copy(
                    src_ref=send_sums.at[source],
                    dst_ref=recv_sums.at[my_batch, my_table],
                    send_sem=send_sems.at[2],
                    recv_sem=sums_sem,
                    device_id=(source % tables, source // tables),
                    device_id_type=MESH,
                ).start()

    recv_sums[my_batch, my_table] = send_sums[me]
    last = recv_weights[0, pl.ds(2 * halves - 1, 1), :]
    for source in range(1, devices):
        last = jnp.maximum(last, recv_weights[source, pl.ds(2 * halves - 1, 1), :])
    flag_ref[0] = jnp.max(jnp.where(lane1 == LANES - 1, last, 0))
    scales = []
    for k in range(tables):
        lengths = jnp.zeros((samples, LANES), jnp.int32)
        for bag in range(short_dev):
            lengths = jnp.where(
                sample_rows == short_sample_ref[k, bag], short_len_ref[k, bag], lengths
            )
        for bag in range(long_dev):
            lengths = jnp.where(
                sample_rows == long_sample_ref[bag, k], long_len_ref[bag, k], lengths
            )
        scales.append(jnp.sqrt(lengths.astype(jnp.float32)))

    arrived(send_sums, sums_sem, devices - 1)

    for k in range(tables):
        total = recv_sums[0, k]
        for s in range(1, batch):
            total = total + recv_sums[s, k]
        out_ref[:, k, :] = total / scales[k]

    arrived(recv_ids, send_sems.at[0], devices - 1)
    arrived(recv_weights, send_sems.at[1], devices - 1)
    arrived(send_sums, send_sems.at[2], devices - 1)


def on_device(emb, short_rows, short_len, short_sample, long_rows, long_len, long_sample):
    tables = lax.axis_size("table")
    batch = lax.axis_size("batch")
    devices = tables * batch
    short_dev, _, short_width = short_rows.shape
    long_dev, _, long_width = long_rows.shape
    rows_dev, width = emb.shape[1:]
    samples = short_dev + long_dev
    slots = capacity_of(short_dev, short_width, long_dev, long_width, batch)
    halves = pl.cdiv(slots, LANES)
    assert width == LANES and rows_dev <= 65536 and rows_dev % (TABLE_CHUNKS * CONVERT_ROWS) == 0
    assert long_width % LANES == 0 and LANES % short_width == 0
    assert devices % GROUP == 0 and tables & (tables - 1) == 0 and batch & (batch - 1) == 0

    smem = pl.BlockSpec(memory_space=pltpu.SMEM)
    vmem = pl.BlockSpec(memory_space=pltpu.VMEM)
    hbm = pl.BlockSpec(memory_space=pl.ANY)
    call = pl.pallas_call(
        functools.partial(pool_kernel, tables, batch, slots),
        out_shape=(
            jax.ShapeDtypeStruct((samples, tables, width), jnp.float32),
            jax.ShapeDtypeStruct((1,), jnp.int32),
        ),
        in_specs=[smem] + [hbm] * 7,
        out_specs=(vmem, smem),
        scratch_shapes=[
            pltpu.VMEM(short_rows.shape, jnp.int32),
            pltpu.SMEM((tables, short_dev), jnp.int32),
            pltpu.SMEM((tables, short_dev), jnp.int32),
            pltpu.VMEM(long_rows.shape, jnp.int32),
            pltpu.SMEM((long_dev, tables), jnp.int32),
            pltpu.SMEM((long_dev, tables), jnp.int32),
            pltpu.VMEM((rows_dev, width), jnp.bfloat16),
            pltpu.VMEM((rows_dev, width), jnp.float32),
            pltpu.VMEM((batch, tables, halves, LANES), jnp.int32),
            pltpu.VMEM((batch, tables, 2 * halves, LANES), jnp.int32),
            pltpu.SMEM((devices, halves, LANES), jnp.int32),
            pltpu.VMEM((devices, 2 * halves, LANES), jnp.int32),
            pltpu.VMEM((2, GROUP, slots, width), jnp.float32),
            pltpu.VMEM((devices, samples, width), jnp.float32),
            pltpu.VMEM((batch, tables, samples, width), jnp.float32),
            pltpu.SemaphoreType.DMA((6,)),
            pltpu.SemaphoreType.DMA((TABLE_CHUNKS,)),
            pltpu.SemaphoreType.DMA((3,)),
            pltpu.SemaphoreType.DMA((devices // GROUP,)),
            pltpu.SemaphoreType.DMA((devices // GROUP,)),
            pltpu.SemaphoreType.DMA,
        ],
        compiler_params=pltpu.CompilerParams(
            collective_id=0, has_side_effects=True, vmem_limit_bytes=56 * 2**20
        ),
        name="pool",
    )

    def run(index):
        return call(
            jnp.full((1,), index, jnp.int32),
            emb,
            short_rows,
            short_len.T,
            short_sample.T,
            long_rows,
            long_len,
            long_sample,
        )

    rounds = pl.cdiv(short_dev * short_width + long_dev * long_width, slots)
    pooled, flag = run(0)
    return lax.cond(
        flag[0] > 0,
        lambda value: lax.fori_loop(1, rounds, lambda r, acc: acc + run(r)[0], value),
        lambda value: value,
        pooled,
    )


def solution(mesh):
    return jax.shard_map(
        on_device,
        mesh=mesh,
        in_specs=(
            P("table", "batch", None),
            P(("table", "batch"), None, None),
            P(("table", "batch"), None),
            P(("table", "batch"), None),
            P(("table", "batch"), None, None),
            P(("table", "batch"), None),
            P(("table", "batch"), None),
        ),
        out_specs=P(("table", "batch"), None, None),
        check_vma=False,
    )
```

time: 27.6 us -> 19.6 us (0.71)
  the two profiles are of different devices: /device:TPU:1 before, /device:TPU:0 now
where the time goes in v2:
time: 19.6 us; the launch traced here: 19.4 us
  Pallas kernels  17.9 us (91%)
  between operations  0.71 us (4%)
  local copies, waits for them, and re-layouts  0.63 us (3%)
    pallas_call x1, Pallas kernels, run(): call(jnp.full((1,), index, jnp.int32), emb, short_rows, short_len.T, shor...  17.9 us
    unnamed x13, local copies, waits for them, and re-layouts  0.63 us

profile of v2, /device:TPU:0, one launch (start us, length us, event | category | flops | bytes accessed | tf_op | source)
XLA Modules:
  0.0 19.4 jit_solution(66317352349100061)
XLA Ops:
  0.0 0.0 copy-start.5
  0.0 0.0 copy-start.4
  0.0 0.0 copy-start
  0.0 0.0 copy-start.3
  0.0 0.0 copy-start.2
  0.0 0.0 copy-start.1
  0.0 17.9 %pool.6 = (f32[8,4,128]{2,1,0:T(4,128)S(1)}, s32[1]{0:T(128)}) custom-call(s32[1]{0:T(128)} %constant.16.clone.1.round_ref, bf16[1,32768,128]{2,1,0:T(8,128)(2,1)} %emb_ref.1, s32[6,4,32]{2,1,0:T(4,128)} %short_rows_hbm.1, s32[4,6]{1,0:T(4,128)} %bitcast.12, s32[4,6]{1,0:T(4,128)} %bitcast.14, s32[2,4,512]{2,1,0:T(4,128)} %long_rows_hbm.1, ...), custom_call_target="tpu_custom_call" | custom-call | tf_op jit(solution)/shard_map/pool/pallas_call | solution.py:411
  18.6 0.0 copy-done.5
  18.6 0.0 copy-done.4
  18.6 0.0 copy-done
  18.6 0.0 copy-done.3
  18.6 0.0 copy-done.2
  18.6 0.0 copy-done.1
  18.6 0.2 conditional.1
  18.8 0.6 %copy.21 = f32[8,4,128]{2,1,0:T(4,128)} copy(f32[8,4,128]{2,1,0:T(4,128)S(1)} %get-tuple-element.182) | data formatting | bytes 32768
Async XLA Ops:
  0.0 18.6 %copy-start.5 = (s32[2,4]{1,0:T(2,128)S(1)}, s32[2,4]{1,0:T(2,128)}, u32[]{:S(2)}) copy-start(s32[2,4]{1,0:T(2,128)} %long_sample_hbm.1) | copy-start | bytes 100
  0.0 18.6 %copy-start.4 = (s32[2,4]{1,0:T(2,128)S(1)}, s32[2,4]{1,0:T(2,128)}, u32[]{:S(2)}) copy-start(s32[2,4]{1,0:T(2,128)} %long_len_hbm.1) | copy-start | bytes 100
  0.0 18.6 %copy-start = (s32[2,4,512]{2,1,0:T(4,128)S(1)}, s32[2,4,512]{2,1,0:T(4,128)}, u32[]{:S(2)}) copy-start(s32[2,4,512]{2,1,0:T(4,128)} %long_rows_hbm.1) | copy-start | bytes 49156
  0.0 18.6 %copy-start.3 = (s32[6,4]{0,1:T(4,128)S(1)}, s32[6,4]{0,1:T(4,128)}, u32[]{:S(2)}) copy-start(s32[6,4]{0,1:T(4,128)} %param.14) | copy-start | bytes 292
  0.0 18.6 %copy-start.2 = (s32[6,4]{0,1:T(4,128)S(1)}, s32[6,4]{0,1:T(4,128)}, u32[]{:S(2)}) copy-start(s32[6,4]{0,1:T(4,128)} %param.13) | copy-start | bytes 292
  0.0 18.6 %copy-start.1 = (s32[6,4,32]{2,1,0:T(4,128)S(1)}, s32[6,4,32]{2,1,0:T(4,128)}, u32[]{:S(2)}) copy-start(s32[6,4,32]{2,1,0:T(4,128)} %short_rows_hbm.1) | copy-start | bytes 9220

commit v3 on v2

--- a/solution.py
+++ b/solution.py
@@ -4,6 +4,7 @@
 import jax
 import jax.numpy as jnp
 from jax import lax
+from jax._src.lax.control_flow.conditionals import cond_p
 from jax.experimental import pallas as pl
 from jax.experimental.pallas import tpu as pltpu
 from jax.sharding import PartitionSpec as P
@@ -11,6 +12,7 @@
 MESH = pl.DeviceIdType.MESH
 LANES = 128
 GROUP = 8
+BATCHED = 4
 TABLE_CHUNKS = 8
 CONVERT_ROWS = 512
 
@@ -19,6 +21,17 @@
     mean = (short_dev * short_width + long_dev * long_width) / batch
     slots = math.ceil((mean + 3.2 * math.sqrt(mean)) / 16) * 16
     return slots - 16 if slots % LANES == 0 else slots
+
+
+def plan_spans(devices):
+    spans = []
+    for group in range(devices // GROUP):
+        begin = group * GROUP
+        if group in (1, 2):
+            spans += [(begin, BATCHED), (begin + BATCHED, GROUP - BATCHED)]
+        else:
+            spans.append((begin, GROUP))
+    return spans
 
 
 def pool_kernel(
@@ -50,12 +63,14 @@
     picked,
     send_sums,
     recv_sums,
+    flag_out,
     input_sems,
     table_sems,
     send_sems,
     ids_sems,
     weights_sems,
     sums_sem,
+    flag_sem,
 ):
     devices = tables * batch
     short_dev, _, short_width = short_rows_ref.shape
@@ -63,10 +78,29 @@
     rows_dev = table.shape[0]
     samples = out_ref.shape[0]
     halves = pl.cdiv(slots, LANES)
-    groups = devices // GROUP
     my_table = lax.axis_index("table")
     my_batch = lax.axis_index("batch")
     me = my_batch * tables + my_table
+    my_group, my_place = me // GROUP, me % GROUP
+
+    def slot_at(step):
+        group, place = step // GROUP, step % GROUP
+        if group == 0:
+            return step
+        if group == 1:
+            return GROUP + my_place
+        return (group // 2 * 2 + my_group % 2) * GROUP + my_place
+
+    def source_of(slot):
+        group, place = slot // GROUP, slot % GROUP
+        if group == 0:
+            return partner(slot)
+        if group == 1:
+            other = my_group ^ 1
+        else:
+            other = (my_group // 2 ^ group // 2) * 2 + group % 2
+        index = other * GROUP + place
+        return index % tables, index // tables
 
     def partner(step):
         return my_table ^ (step % tables), my_batch ^ (step // tables)
@@ -238,31 +272,30 @@
             send_weights[:, k, halves + h, :] = count
 
     pl.semaphore_wait(barrier, devices - 1)
-    my_group = me // GROUP
     for step in reversed(range(1, devices)):
         to_table, to_batch = partner(step)
         pltpu.make_async_remote_copy(
             src_ref=send_ids.at[to_batch, to_table],
-            dst_ref=recv_ids.at[me],
+            dst_ref=recv_ids.at[slot_at(step)],
             send_sem=send_sems.at[0],
-            recv_sem=ids_sems.at[my_group],
+            recv_sem=ids_sems.at[slot_at(step) // BATCHED],
             device_id=(to_table, to_batch),
             device_id_type=MESH,
         ).start()
     pltpu.make_async_copy(
-        send_ids.at[my_batch, my_table], recv_ids.at[me], ids_sems.at[my_group]
+        send_ids.at[my_batch, my_table], recv_ids.at[0], ids_sems.at[0]
     ).start()
     for step in reversed(range(1, devices)):
         to_table, to_batch = partner(step)
         pltpu.make_async_remote_copy(
             src_ref=send_weights.at[to_batch, to_table],
-            dst_ref=recv_weights.at[me],
+            dst_ref=recv_weights.at[slot_at(step)],
             send_sem=send_sems.at[1],
-            recv_sem=weights_sems.at[my_group],
+            recv_sem=weights_sems.at[slot_at(step) // BATCHED],
             device_id=(to_table, to_batch),
             device_id_type=MESH,
         ).start()
-    recv_weights[me] = send_weights[my_batch, my_table]
+    recv_weights[0] = send_weights[my_batch, my_table]
 
     for index in range(TABLE_CHUNKS):
         table_copy(index).wait()
@@ -280,23 +313,18 @@
         pltpu.make_async_copy(ref.at[pl.ds(0, count)], ref.at[pl.ds(0, count)], sem).wait()
 
     sample_rows = lax.broadcasted_iota(jnp.int32, (samples, LANES), 0)
-    for group in range(groups):
-        begin = group * GROUP
-        arrived(recv_ids, ids_sems.at[group], GROUP)
-        for step in range(GROUP):
+    for group, (begin, size) in enumerate(plan_spans(devices)):
+        for first_slot in range(begin, begin + size, BATCHED):
+            arrived(recv_ids, ids_sems.at[first_slot // BATCHED], BATCHED)
+        for step in range(size):
             for slot in range(slots):
                 row = recv_ids[begin + step, slot // LANES, slot % LANES]
                 picked[group % 2, step, pl.ds(slot, 1), :] = table[pl.ds(row, 1), :]
-
-        @pl.when(my_group == group)
-        def _():
-            arrived(recv_weights, weights_sems.at[group], GROUP - 1)
-
-        @pl.when(my_group != group)
-        def _():
-            arrived(recv_weights, weights_sems.at[group], GROUP)
-
-        for step in range(GROUP):
+        for first_slot in range(begin, begin + size, BATCHED):
+            count = BATCHED - 1 if first_slot == 0 else BATCHED
+            arrived(recv_weights, weights_sems.at[first_slot // BATCHED], count)
+
+        for step in range(size):
             weights = []
             for h in range(halves):
                 sample = recv_weights[begin + step, pl.ds(h, 1), :]
@@ -308,25 +336,23 @@
                 picked[group % 2, step].astype(jnp.bfloat16),
                 preferred_element_type=jnp.float32,
             )
-        for step in range(GROUP):
-            source = begin + step
-
-            @pl.when(me != source)
-            def _():
-                pltpu.make_async_remote_copy(
-                    src_ref=send_sums.at[source],
-                    dst_ref=recv_sums.at[my_batch, my_table],
-                    send_sem=send_sems.at[2],
-                    recv_sem=sums_sem,
-                    device_id=(source % tables, source // tables),
-                    device_id_type=MESH,
-                ).start()
-
-    recv_sums[my_batch, my_table] = send_sums[me]
+        for step in range(max(begin, 1), begin + size):
+            pltpu.make_async_remote_copy(
+                src_ref=send_sums.at[step],
+                dst_ref=recv_sums.at[my_batch, my_table],
+                send_sem=send_sems.at[2],
+                recv_sem=sums_sem,
+                device_id=source_of(step),
+                device_id_type=MESH,
+            ).start()
+
+    recv_sums[my_batch, my_table] = send_sums[0]
     last = recv_weights[0, pl.ds(2 * halves - 1, 1), :]
     for source in range(1, devices):
         last = jnp.maximum(last, recv_weights[source, pl.ds(2 * halves - 1, 1), :])
-    flag_ref[0] = jnp.max(jnp.where(lane1 == LANES - 1, last, 0))
+    flag_out[...] = jnp.broadcast_to(jnp.max(jnp.where(lane1 == LANES - 1, last, 0)), (LANES,))
+    flag_copy = pltpu.make_async_copy(flag_out, flag_ref, flag_sem)
+    flag_copy.start()
     scales = []
     for k in range(tables):
         lengths = jnp.zeros((samples, LANES), jnp.int32)
@@ -348,9 +374,15 @@
             total = total + recv_sums[s, k]
         out_ref[:, k, :] = total / scales[k]
 
+    flag_copy.wait()
     arrived(recv_ids, send_sems.at[0], devices - 1)
     arrived(recv_weights, send_sems.at[1], devices - 1)
     arrived(send_sums, send_sems.at[2], devices - 1)
+
+
+def choose(index, first, second, *operands):
+    branches = tuple(jax.make_jaxpr(branch)(*operands) for branch in (first, second))
+    return cond_p.bind(index, *operands, branches=branches)[0]
 
 
 def on_device(emb, short_rows, short_len, short_sample, long_rows, long_len, long_sample):
@@ -374,10 +406,10 @@
         functools.partial(pool_kernel, tables, batch, slots),
         out_shape=(
             jax.ShapeDtypeStruct((samples, tables, width), jnp.float32),
-            jax.ShapeDtypeStruct((1,), jnp.int32),
+            pltpu.SMEM((128,), jnp.int32),
         ),
         in_specs=[smem] + [hbm] * 7,
-        out_specs=(vmem, smem),
+        out_specs=(vmem, hbm),
         scratch_shapes=[
             pltpu.VMEM(short_rows.shape, jnp.int32),
             pltpu.SMEM((tables, short_dev), jnp.int32),
@@ -394,11 +426,13 @@
             pltpu.VMEM((2, GROUP, slots, width), jnp.float32),
             pltpu.VMEM((devices, samples, width), jnp.float32),
             pltpu.VMEM((batch, tables, samples, width), jnp.float32),
+            pltpu.VMEM((128,), jnp.int32),
             pltpu.SemaphoreType.DMA((6,)),
             pltpu.SemaphoreType.DMA((TABLE_CHUNKS,)),
             pltpu.SemaphoreType.DMA((3,)),
-            pltpu.SemaphoreType.DMA((devices // GROUP,)),
-            pltpu.SemaphoreType.DMA((devices // GROUP,)),
+            pltpu.SemaphoreType.DMA((devices // BATCHED,)),
+            pltpu.SemaphoreType.DMA((devices // BATCHED,)),
+            pltpu.SemaphoreType.DMA,
             pltpu.SemaphoreType.DMA,
         ],
         compiler_params=pltpu.CompilerParams(
@@ -407,26 +441,21 @@
         name="pool",
     )
 
-    def run(index):
-        return call(
-            jnp.full((1,), index, jnp.int32),
-            emb,
-            short_rows,
-            short_len.T,
-            short_sample.T,
-            long_rows,
-            long_len,
-            long_sample,
-        )
-
-    rounds = pl.cdiv(short_dev * short_width + long_dev * long_width, slots)
-    pooled, flag = run(0)
-    return lax.cond(
-        flag[0] > 0,
-        lambda value: lax.fori_loop(1, rounds, lambda r, acc: acc + run(r)[0], value),
-        lambda value: value,
-        pooled,
-    )
+    def run(index, operands):
+        return call(jnp.reshape(jnp.asarray(index, jnp.int32), (1,)), *operands)
+
+    def rounds(pooled, *operands):
+        def again(state):
+            index, _, pooled = state
+            more, flag = run(index, operands)
+            return index + 1, flag[0], pooled + more
+
+        state = (jnp.int32(1), jnp.int32(1), pooled)
+        return lax.while_loop(lambda state: state[1] > 0, again, state)[2]
+
+    operands = (emb, short_rows, short_len.T, short_sample.T, long_rows, long_len, long_sample)
+    pooled, flag = run(0, operands)
+    return choose(flag[0], lambda value, *_: value, rounds, pooled, *operands)
 
 
 def solution(mesh):

time: 19.6 us -> 18 us (0.918)
  Pallas kernels: 17.9 us -> 17 us
  between operations: 0.71 us -> 0.08 us
    pallas_call x1, Pallas kernels: 17.9 us -> 17 us  [run(): return call(jnp.reshape(jnp.asarray(index, jnp.int32), (1,)), *operands)]
where the time goes in v3:
time: 18 us; the launch traced here: 17.9 us
  Pallas kernels  17 us (94%)
  local copies, waits for them, and re-layouts  0.63 us (4%)
  loops' own time  0.23 us (1%)
    pallas_call x1, Pallas kernels, run(): return call(jnp.reshape(jnp.asarray(index, jnp.int32), (1,)), *operands)  17 us
    unnamed x13, local copies, waits for them, and re-layouts  0.63 us

profile of v3, /device:TPU:0, one launch (start us, length us, event | category | flops | bytes accessed | tf_op | source)
XLA Modules:
  0.0 17.9 jit_solution(2386384313351176977)
XLA Ops:
  0.0 0.0 copy-start.5
  0.0 0.0 copy-start.4
  0.0 0.0 copy-start
  0.0 0.0 copy-start.1
  0.0 0.0 copy-start.3
  0.0 0.0 copy-start.2
  0.0 17.0 %pool.2 = (f32[8,4,128]{2,1,0:T(4,128)S(1)}, s32[128]{0:T(128)S(4)}) custom-call(s32[1]{0:T(128)} %constant.4.clone.1.round_ref, bf16[1,32768,128]{2,1,0:T(8,128)(2,1)} %emb_ref.1, s32[6,4,32]{2,1,0:T(4,128)} %short_rows_hbm.1, s32[4,6]{1,0:T(4,128)} %bitcast.13, s32[4,6]{1,0:T(4,128)} %bitcast.15, s32[2,4,512]{2,1,0:T(4,128)} %long_rows_hbm.1, ...), custom_call_target="tpu_custom_call" | custom-call | tf_op jit(solution)/shard_map/pool/pallas_call | solution.py:445
  17.0 0.0 copy-done.5
  17.0 0.0 copy-done.4
  17.0 0.0 copy-done
  17.0 0.0 copy-done.1
  17.0 0.0 copy-done.3
  17.0 0.0 copy-done.2
  17.0 0.2 %conditional.1 = (f32[8,4,128]{2,1,0:T(4,128)S(1)}) conditional(s32[]{:T(128)S(4)} %bitcast.4, f32[8,4,128]{2,1,0:T(4,128)S(1)} %get-tuple-element.89, (bf16[1,32768,128]{2,1,0:T(8,128)(2,1)}, s32[6,4,32]{2,1,0:T(4,128)S(1)}, s32[4,6]{1,0:T(4,128)S(1)}, s32[4,6]{1,0:T(4,128)S(1)}, s32[2,4,512]{2,1,0:T(4,128)S(1)}, /*index=5*/s32[2,4]{1,0:T(2,128)S(1)}, ...), branch_computations={%region_0.0_spmd, %region_1.0_spmd} | conditional | flops 4098 | bytes 49381 | solution.py:385
  17.3 0.6 %copy.22 = f32[8,4,128]{2,1,0:T(4,128)} copy(f32[8,4,128]{2,1,0:T(4,128)S(1)} %get-tuple-element.90) | data formatting | bytes 32768
Async XLA Ops:
  0.0 17.0 %copy-start.5 = (s32[2,4]{1,0:T(2,128)S(1)}, s32[2,4]{1,0:T(2,128)}, u32[]{:S(2)}) copy-start(s32[2,4]{1,0:T(2,128)} %long_sample_hbm.1) | copy-start | bytes 100
  0.0 17.0 %copy-start.4 = (s32[2,4]{1,0:T(2,128)S(1)}, s32[2,4]{1,0:T(2,128)}, u32[]{:S(2)}) copy-start(s32[2,4]{1,0:T(2,128)} %long_len_hbm.1) | copy-start | bytes 100
  0.0 17.0 %copy-start = (s32[2,4,512]{2,1,0:T(4,128)S(1)}, s32[2,4,512]{2,1,0:T(4,128)}, u32[]{:S(2)}) copy-start(s32[2,4,512]{2,1,0:T(4,128)} %long_rows_hbm.1) | copy-start | bytes 49156
  0.0 17.0 %copy-start.1 = (s32[6,4,32]{2,1,0:T(4,128)S(1)}, s32[6,4,32]{2,1,0:T(4,128)}, u32[]{:S(2)}) copy-start(s32[6,4,32]{2,1,0:T(4,128)} %short_rows_hbm.1) | copy-start | bytes 9220
  0.0 17.0 %copy-start.3 = (s32[6,4]{0,1:T(4,128)S(1)}, s32[6,4]{0,1:T(4,128)}, u32[]{:S(2)}) copy-start(s32[6,4]{0,1:T(4,128)} %param.14) | copy-start | bytes 292
  0.0 17.0 %copy-start.2 = (s32[6,4]{0,1:T(4,128)S(1)}, s32[6,4]{0,1:T(4,128)}, u32[]{:S(2)}) copy-start(s32[6,4]{0,1:T(4,128)} %param.13) | copy-start | bytes 292

commit v4 on v3

--- a/solution.py
+++ b/solution.py
@@ -11,9 +11,10 @@
 
 MESH = pl.DeviceIdType.MESH
 LANES = 128
+INPUTS = 6
 GROUP = 8
-BATCHED = 4
-TABLE_CHUNKS = 8
+AHEAD = 2
+TABLE_CHUNKS = 2
 CONVERT_ROWS = 512
 
 
@@ -23,14 +24,26 @@
     return slots - 16 if slots % LANES == 0 else slots
 
 
+def parts_of(devices):
+    parts = [(0, GROUP)]
+    for begin in range(GROUP, devices, GROUP):
+        parts += [(begin, AHEAD), (begin + AHEAD, GROUP - AHEAD)]
+    return parts
+
+
+def part_at(group, place):
+    return 2 * group - (GROUP - 1 - place) // (GROUP - AHEAD)
+
+
 def plan_spans(devices):
     spans = []
     for group in range(devices // GROUP):
-        begin = group * GROUP
-        if group in (1, 2):
-            spans += [(begin, BATCHED), (begin + BATCHED, GROUP - BATCHED)]
+        if group == 0:
+            spans.append([0])
+        elif group in (1, 2):
+            spans += [[2 * group - 1], [2 * group]]
         else:
-            spans.append((begin, GROUP))
+            spans.append([2 * group - 1, 2 * group])
     return spans
 
 
@@ -64,13 +77,10 @@
     send_sums,
     recv_sums,
     flag_out,
-    input_sems,
-    table_sems,
-    send_sems,
+    local_sems,
     ids_sems,
     weights_sems,
     sums_sem,
-    flag_sem,
 ):
     devices = tables * batch
     short_dev, _, short_width = short_rows_ref.shape
@@ -86,10 +96,10 @@
     def slot_at(step):
         group, place = step // GROUP, step % GROUP
         if group == 0:
-            return step
-        if group == 1:
-            return GROUP + my_place
-        return (group // 2 * 2 + my_group % 2) * GROUP + my_place
+            return step, 0
+        if group > 1:
+            group = group // 2 * 2 + my_group % 2
+        return group * GROUP + my_place, part_at(group, my_place)
 
     def source_of(slot):
         group, place = slot // GROUP, slot % GROUP
@@ -110,11 +120,11 @@
     def table_copy(index):
         span = pl.ds(index * chunk, chunk)
         return pltpu.make_async_copy(
-            emb_ref.at[0, span, :], table_raw.at[span, :], table_sems.at[index]
+            emb_ref.at[0, span, :], table_raw.at[span, :], local_sems.at[INPUTS + index]
         )
 
     inputs = [
-        pltpu.make_async_copy(source, target, input_sems.at[index])
+        pltpu.make_async_copy(source, target, local_sems.at[index])
         for index, (source, target) in enumerate(
             [
                 (long_rows_hbm, long_rows_ref),
@@ -272,29 +282,28 @@
             send_weights[:, k, halves + h, :] = count
 
     pl.semaphore_wait(barrier, devices - 1)
-    for step in reversed(range(1, devices)):
+    def send_to(step, source, target, kind, sems):
         to_table, to_batch = partner(step)
+        slot, part = slot_at(step)
         pltpu.make_async_remote_copy(
-            src_ref=send_ids.at[to_batch, to_table],
-            dst_ref=recv_ids.at[slot_at(step)],
-            send_sem=send_sems.at[0],
-            recv_sem=ids_sems.at[slot_at(step) // BATCHED],
+            src_ref=source.at[to_batch, to_table],
+            dst_ref=target.at[slot],
+            send_sem=local_sems.at[kind],
+            recv_sem=sems.at[part],
             device_id=(to_table, to_batch),
             device_id_type=MESH,
         ).start()
-    pltpu.make_async_copy(
-        send_ids.at[my_batch, my_table], recv_ids.at[0], ids_sems.at[0]
-    ).start()
-    for step in reversed(range(1, devices)):
-        to_table, to_batch = partner(step)
-        pltpu.make_async_remote_copy(
-            src_ref=send_weights.at[to_batch, to_table],
-            dst_ref=recv_weights.at[slot_at(step)],
-            send_sem=send_sems.at[1],
-            recv_sem=weights_sems.at[slot_at(step) // BATCHED],
-            device_id=(to_table, to_batch),
-            device_id_type=MESH,
-        ).start()
+
+    far = devices - GROUP
+    for steps in (range(far, devices), range(1, far)):
+        for step in reversed(steps):
+            send_to(step, send_ids, recv_ids, 0, ids_sems)
+        if 1 in steps:
+            pltpu.make_async_copy(
+                send_ids.at[my_batch, my_table], recv_ids.at[0], ids_sems.at[0]
+            ).start()
+        for step in reversed(steps):
+            send_to(step, send_weights, recv_weights, 1, weights_sems)
     recv_weights[0] = send_weights[my_batch, my_table]
 
     for index in range(TABLE_CHUNKS):
@@ -313,34 +322,52 @@
         pltpu.make_async_copy(ref.at[pl.ds(0, count)], ref.at[pl.ds(0, count)], sem).wait()
 
     sample_rows = lax.broadcasted_iota(jnp.int32, (samples, LANES), 0)
-    for group, (begin, size) in enumerate(plan_spans(devices)):
-        for first_slot in range(begin, begin + size, BATCHED):
-            arrived(recv_ids, ids_sems.at[first_slot // BATCHED], BATCHED)
-        for step in range(size):
+    def pick(buffer, slots_of):
+        for slot_of in slots_of:
             for slot in range(slots):
-                row = recv_ids[begin + step, slot // LANES, slot % LANES]
-                picked[group % 2, step, pl.ds(slot, 1), :] = table[pl.ds(row, 1), :]
-        for first_slot in range(begin, begin + size, BATCHED):
-            count = BATCHED - 1 if first_slot == 0 else BATCHED
-            arrived(recv_weights, weights_sems.at[first_slot // BATCHED], count)
-
-        for step in range(size):
+                row = recv_ids[slot_of, slot // LANES, slot % LANES]
+                picked[buffer, slot_of % GROUP, pl.ds(slot, 1), :] = table[pl.ds(row, 1), :]
+
+    parts = parts_of(devices)
+
+    def wait_ids(span):
+        for part in span:
+            arrived(recv_ids, ids_sems.at[part], parts[part][1])
+
+    spans = plan_spans(devices)
+    started = 0
+    for index, span in enumerate(spans):
+        begin, size = parts[span[0]][0], sum(parts[part][1] for part in span)
+        buffer = index % 2
+        if not started:
+            wait_ids(span)
+        pick(buffer, range(begin + started, begin + size))
+        for part in span:
+            arrived(recv_weights, weights_sems.at[part], parts[part][1] - (part == 0))
+
+        started = 0
+        if index + 1 < len(spans) and 3 not in span and 3 not in spans[index + 1]:
+            wait_ids(spans[index + 1])
+            following = parts[spans[index + 1][0]][0]
+            started = AHEAD
+            pick(1 - buffer, range(following, following + started))
+        for step in range(begin, begin + size):
             weights = []
             for h in range(halves):
-                sample = recv_weights[begin + step, pl.ds(h, 1), :]
-                count = recv_weights[begin + step, pl.ds(halves + h, 1), :]
+                sample = recv_weights[step, pl.ds(h, 1), :]
+                count = recv_weights[step, pl.ds(halves + h, 1), :]
                 weight = jnp.where(sample_rows == sample, count, 0).astype(jnp.float32)
                 weights.append(weight[:, : min(LANES, slots - h * LANES)])
-            send_sums[begin + step] = jnp.dot(
+            send_sums[step] = jnp.dot(
                 jnp.concatenate(weights, axis=1).astype(jnp.bfloat16),
-                picked[group % 2, step].astype(jnp.bfloat16),
+                picked[buffer, step % GROUP].astype(jnp.bfloat16),
                 preferred_element_type=jnp.float32,
             )
         for step in range(max(begin, 1), begin + size):
             pltpu.make_async_remote_copy(
                 src_ref=send_sums.at[step],
                 dst_ref=recv_sums.at[my_batch, my_table],
-                send_sem=send_sems.at[2],
+                send_sem=local_sems.at[2],
                 recv_sem=sums_sem,
                 device_id=source_of(step),
                 device_id_type=MESH,
@@ -351,7 +378,7 @@
     for source in range(1, devices):
         last = jnp.maximum(last, recv_weights[source, pl.ds(2 * halves - 1, 1), :])
     flag_out[...] = jnp.broadcast_to(jnp.max(jnp.where(lane1 == LANES - 1, last, 0)), (LANES,))
-    flag_copy = pltpu.make_async_copy(flag_out, flag_ref, flag_sem)
+    flag_copy = pltpu.make_async_copy(flag_out, flag_ref, local_sems.at[3])
     flag_copy.start()
     scales = []
     for k in range(tables):
@@ -375,9 +402,9 @@
         out_ref[:, k, :] = total / scales[k]
 
     flag_copy.wait()
-    arrived(recv_ids, send_sems.at[0], devices - 1)
-    arrived(recv_weights, send_sems.at[1], devices - 1)
-    arrived(send_sums, send_sems.at[2], devices - 1)
+    arrived(recv_ids, local_sems.at[0], devices - 1)
+    arrived(recv_weights, local_sems.at[1], devices - 1)
+    arrived(send_sums, local_sems.at[2], devices - 1)
 
 
 def choose(index, first, second, *operands):
@@ -427,12 +454,9 @@
             pltpu.VMEM((devices, samples, width), jnp.float32),
             pltpu.VMEM((batch, tables, samples, width), jnp.float32),
             pltpu.VMEM((128,), jnp.int32),
-            pltpu.SemaphoreType.DMA((6,)),
-            pltpu.SemaphoreType.DMA((TABLE_CHUNKS,)),
-            pltpu.SemaphoreType.DMA((3,)),
-            pltpu.SemaphoreType.DMA((devices // BATCHED,)),
-            pltpu.SemaphoreType.DMA((devices // BATCHED,)),
-            pltpu.SemaphoreType.DMA,
+            pltpu.SemaphoreType.DMA((INPUTS + TABLE_CHUNKS,)),
+            pltpu.SemaphoreType.DMA((devices // GROUP * 2 - 1,)),
+            pltpu.SemaphoreType.DMA((devices // GROUP * 2 - 1,)),
             pltpu.SemaphoreType.DMA,
         ],
         compiler_params=pltpu.CompilerParams(

time: 18 us -> 17.8 us (0.989)
  Pallas kernels: 17 us -> 16.7 us
    pallas_call x1, Pallas kernels: 17 us -> 16.7 us  [run(): return call(jnp.reshape(jnp.asarray(index, jnp.int32), (1,)), *operands)]
where the time goes in v4:
time: 17.8 us; the launch traced here: 17.6 us
  Pallas kernels  16.7 us (94%)
  local copies, waits for them, and re-layouts  0.63 us (4%)
  loops' own time  0.23 us (1%)
    pallas_call x1, Pallas kernels, run(): return call(jnp.reshape(jnp.asarray(index, jnp.int32), (1,)), *operands)  16.7 us
    unnamed x13, local copies, waits for them, and re-layouts  0.63 us

profile of v4, /device:TPU:0, one launch (start us, length us, event | category | flops | bytes accessed | tf_op | source)
XLA Modules:
  0.0 17.6 jit_solution(6943264997378416405)
XLA Ops:
  0.0 0.0 copy-start.5
  0.0 0.0 copy-start.4
  0.0 0.0 copy-start
  0.0 0.0 copy-start.1
  0.0 0.0 copy-start.3
  0.0 0.0 copy-start.2
  0.0 16.7 %pool.2 = (f32[8,4,128]{2,1,0:T(4,128)S(1)}, s32[128]{0:T(128)S(4)}) custom-call(s32[1]{0:T(128)} %constant.4.clone.1.round_ref, bf16[1,32768,128]{2,1,0:T(8,128)(2,1)} %emb_ref.1, s32[6,4,32]{2,1,0:T(4,128)} %short_rows_hbm.1, s32[4,6]{1,0:T(4,128)} %bitcast.13, s32[4,6]{1,0:T(4,128)} %bitcast.15, s32[2,4,512]{2,1,0:T(4,128)} %long_rows_hbm.1, ...), custom_call_target="tpu_custom_call" | custom-call | tf_op jit(solution)/shard_map/pool/pallas_call | solution.py:469
  16.7 0.0 copy-done.5
  16.7 0.0 copy-done.4
  16.7 0.0 copy-done
  16.8 0.0 copy-done.1
  16.8 0.0 copy-done.3
  16.8 0.0 copy-done.2
  16.8 0.2 %conditional.1 = (f32[8,4,128]{2,1,0:T(4,128)S(1)}) conditional(s32[]{:T(128)S(4)} %bitcast.4, f32[8,4,128]{2,1,0:T(4,128)S(1)} %get-tuple-element.89, (bf16[1,32768,128]{2,1,0:T(8,128)(2,1)}, s32[6,4,32]{2,1,0:T(4,128)S(1)}, s32[4,6]{1,0:T(4,128)S(1)}, s32[4,6]{1,0:T(4,128)S(1)}, s32[2,4,512]{2,1,0:T(4,128)S(1)}, /*index=5*/s32[2,4]{1,0:T(2,128)S(1)}, ...), branch_computations={%region_0.0_spmd, %region_1.0_spmd} | conditional | flops 4098 | bytes 49381 | solution.py:412
  17.0 0.6 %copy.22 = f32[8,4,128]{2,1,0:T(4,128)} copy(f32[8,4,128]{2,1,0:T(4,128)S(1)} %get-tuple-element.90) | data formatting | bytes 32768
Async XLA Ops:
  0.0 16.7 %copy-start.5 = (s32[2,4]{1,0:T(2,128)S(1)}, s32[2,4]{1,0:T(2,128)}, u32[]{:S(2)}) copy-start(s32[2,4]{1,0:T(2,128)} %long_sample_hbm.1) | copy-start | bytes 100
  0.0 16.7 %copy-start.4 = (s32[2,4]{1,0:T(2,128)S(1)}, s32[2,4]{1,0:T(2,128)}, u32[]{:S(2)}) copy-start(s32[2,4]{1,0:T(2,128)} %long_len_hbm.1) | copy-start | bytes 100
  0.0 16.7 %copy-start = (s32[2,4,512]{2,1,0:T(4,128)S(1)}, s32[2,4,512]{2,1,0:T(4,128)}, u32[]{:S(2)}) copy-start(s32[2,4,512]{2,1,0:T(4,128)} %long_rows_hbm.1) | copy-start | bytes 49156
  0.0 16.7 %copy-start.1 = (s32[6,4,32]{2,1,0:T(4,128)S(1)}, s32[6,4,32]{2,1,0:T(4,128)}, u32[]{:S(2)}) copy-start(s32[6,4,32]{2,1,0:T(4,128)} %short_rows_hbm.1) | copy-start | bytes 9220
  0.0 16.8 %copy-start.3 = (s32[6,4]{0,1:T(4,128)S(1)}, s32[6,4]{0,1:T(4,128)}, u32[]{:S(2)}) copy-start(s32[6,4]{0,1:T(4,128)} %param.14) | copy-start | bytes 292
  0.0 16.8 %copy-start.2 = (s32[6,4]{0,1:T(4,128)S(1)}, s32[6,4]{0,1:T(4,128)}, u32[]{:S(2)}) copy-start(s32[6,4]{0,1:T(4,128)} %param.13) | copy-start | bytes 292

commit v5 on v4

--- a/solution.py
+++ b/solution.py
@@ -136,11 +136,14 @@
             ]
         )
     ]
-    for copy in inputs:
-        copy.start()
     barrier = pltpu.get_barrier_semaphore()
-    for step in reversed(range(1, devices)):
-        pl.semaphore_signal(barrier, inc=1, device_id=partner(step), device_id_type=MESH)
+    far = devices - GROUP
+    for steps in (range(far, devices), range(1, far)):
+        for step in reversed(steps):
+            pl.semaphore_signal(barrier, inc=1, device_id=partner(step), device_id_type=MESH)
+        if far in steps:
+            for copy in inputs:
+                copy.start()
     for index in range(TABLE_CHUNKS):
         table_copy(index).start()
     for copy in inputs:
@@ -294,7 +297,6 @@
             device_id_type=MESH,
         ).start()
 
-    far = devices - GROUP
     for steps in (range(far, devices), range(1, far)):
         for step in reversed(steps):
             send_to(step, send_ids, recv_ids, 0, ids_sems)
@@ -334,24 +336,8 @@
         for part in span:
             arrived(recv_ids, ids_sems.at[part], parts[part][1])
 
-    spans = plan_spans(devices)
-    started = 0
-    for index, span in enumerate(spans):
-        begin, size = parts[span[0]][0], sum(parts[part][1] for part in span)
-        buffer = index % 2
-        if not started:
-            wait_ids(span)
-        pick(buffer, range(begin + started, begin + size))
-        for part in span:
-            arrived(recv_weights, weights_sems.at[part], parts[part][1] - (part == 0))
-
-        started = 0
-        if index + 1 < len(spans) and 3 not in span and 3 not in spans[index + 1]:
-            wait_ids(spans[index + 1])
-            following = parts[spans[index + 1][0]][0]
-            started = AHEAD
-            pick(1 - buffer, range(following, following + started))
-        for step in range(begin, begin + size):
+    def multiply(buffer, steps):
+        for step in steps:
             weights = []
             for h in range(halves):
                 sample = recv_weights[step, pl.ds(h, 1), :]
@@ -363,7 +349,11 @@
                 picked[buffer, step % GROUP].astype(jnp.bfloat16),
                 preferred_element_type=jnp.float32,
             )
-        for step in range(max(begin, 1), begin + size):
+
+    def answer(steps):
+        for step in steps:
+            if step == 0:
+                continue
             pltpu.make_async_remote_copy(
                 src_ref=send_sums.at[step],
                 dst_ref=recv_sums.at[my_batch, my_table],
@@ -372,6 +362,32 @@
                 device_id=source_of(step),
                 device_id_type=MESH,
             ).start()
+
+    spans = plan_spans(devices)
+    started = 0
+    for index, span in enumerate(spans):
+        begin, size = parts[span[0]][0], sum(parts[part][1] for part in span)
+        buffer = index % 2
+        if not started:
+            wait_ids(span)
+        now = 1 if 3 in span else size
+        pick(buffer, range(begin + started, begin + now))
+        for part in span:
+            arrived(recv_weights, weights_sems.at[part], parts[part][1] - (part == 0))
+        pick(buffer, range(begin + now, begin + size))
+
+        started = 0
+        if index + 1 < len(spans) and 3 not in span and 3 not in spans[index + 1]:
+            wait_ids(spans[index + 1])
+            following = parts[spans[index + 1][0]][0]
+            started = AHEAD
+            pick(1 - buffer, range(following, following + started))
+        if 3 in span:
+            multiply(buffer, [begin])
+            answer([begin])
+            begin, size = begin + 1, size - 1
+        multiply(buffer, range(begin, begin + size))
+        answer(range(begin, begin + size))
 
     recv_sums[my_batch, my_table] = send_sums[0]
     last = recv_weights[0, pl.ds(2 * halves - 1, 1), :]

time: 17.8 us -> 17.7 us (level)
  no operation moved by 1% of the time
where the time goes in v5:
time: 17.7 us; the launch traced here: 17.6 us
  Pallas kernels  16.6 us (94%)
  local copies, waits for them, and re-layouts  0.63 us (4%)
  loops' own time  0.23 us (1%)
    pallas_call x1, Pallas kernels, run(): return call(jnp.reshape(jnp.asarray(index, jnp.int32), (1,)), *operands)  16.6 us
    unnamed x13, local copies, waits for them, and re-layouts  0.63 us

profile of v5, /device:TPU:0, one launch (start us, length us, event | category | flops | bytes accessed | tf_op | source)
XLA Modules:
  0.0 17.6 jit_solution(3974137661616089890)
XLA Ops:
  0.0 0.0 copy-start.5
  0.0 0.0 copy-start.4
  0.0 0.0 copy-start
  0.0 0.0 copy-start.1
  0.0 0.0 copy-start.3
  0.0 0.0 copy-start.2
  0.0 16.6 %pool.2 = (f32[8,4,128]{2,1,0:T(4,128)S(1)}, s32[128]{0:T(128)S(4)}) custom-call(s32[1]{0:T(128)} %constant.4.clone.1.round_ref, bf16[1,32768,128]{2,1,0:T(8,128)(2,1)} %emb_ref.1, s32[6,4,32]{2,1,0:T(4,128)} %short_rows_hbm.1, s32[4,6]{1,0:T(4,128)} %bitcast.13, s32[4,6]{1,0:T(4,128)} %bitcast.15, s32[2,4,512]{2,1,0:T(4,128)} %long_rows_hbm.1, ...), custom_call_target="tpu_custom_call" | custom-call | tf_op jit(solution)/shard_map/pool/pallas_call | solution.py:485
  16.7 0.0 copy-done.5
  16.7 0.0 copy-done.4
  16.7 0.0 copy-done
  16.7 0.0 copy-done.1
  16.7 0.0 copy-done.3
  16.7 0.0 copy-done.2
  16.7 0.2 %conditional.1 = (f32[8,4,128]{2,1,0:T(4,128)S(1)}) conditional(s32[]{:T(128)S(4)} %bitcast.4, f32[8,4,128]{2,1,0:T(4,128)S(1)} %get-tuple-element.89, (bf16[1,32768,128]{2,1,0:T(8,128)(2,1)}, s32[6,4,32]{2,1,0:T(4,128)S(1)}, s32[4,6]{1,0:T(4,128)S(1)}, s32[4,6]{1,0:T(4,128)S(1)}, s32[2,4,512]{2,1,0:T(4,128)S(1)}, /*index=5*/s32[2,4]{1,0:T(2,128)S(1)}, ...), branch_computations={%region_0.0_spmd, %region_1.0_spmd} | conditional | flops 4098 | bytes 49381 | solution.py:428
  17.0 0.6 %copy.22 = f32[8,4,128]{2,1,0:T(4,128)} copy(f32[8,4,128]{2,1,0:T(4,128)S(1)} %get-tuple-element.90) | data formatting | bytes 32768
Async XLA Ops:
  0.0 16.7 %copy-start.5 = (s32[2,4]{1,0:T(2,128)S(1)}, s32[2,4]{1,0:T(2,128)}, u32[]{:S(2)}) copy-start(s32[2,4]{1,0:T(2,128)} %long_sample_hbm.1) | copy-start | bytes 100
  0.0 16.7 %copy-start.4 = (s32[2,4]{1,0:T(2,128)S(1)}, s32[2,4]{1,0:T(2,128)}, u32[]{:S(2)}) copy-start(s32[2,4]{1,0:T(2,128)} %long_len_hbm.1) | copy-start | bytes 100
  0.0 16.7 %copy-start = (s32[2,4,512]{2,1,0:T(4,128)S(1)}, s32[2,4,512]{2,1,0:T(4,128)}, u32[]{:S(2)}) copy-start(s32[2,4,512]{2,1,0:T(4,128)} %long_rows_hbm.1) | copy-start | bytes 49156
  0.0 16.7 %copy-start.1 = (s32[6,4,32]{2,1,0:T(4,128)S(1)}, s32[6,4,32]{2,1,0:T(4,128)}, u32[]{:S(2)}) copy-start(s32[6,4,32]{2,1,0:T(4,128)} %short_rows_hbm.1) | copy-start | bytes 9220
  0.0 16.7 %copy-start.3 = (s32[6,4]{0,1:T(4,128)S(1)}, s32[6,4]{0,1:T(4,128)}, u32[]{:S(2)}) copy-start(s32[6,4]{0,1:T(4,128)} %param.14) | copy-start | bytes 292
  0.0 16.7 %copy-start.2 = (s32[6,4]{0,1:T(4,128)S(1)}, s32[6,4]{0,1:T(4,128)}, u32[]{:S(2)}) copy-start(s32[6,4]{0,1:T(4,128)} %param.13) | copy-start | bytes 292
